TPU v7x, 128 devices: a 2x2x16 block of a 8x8x16 slice. The times are simulated.
128 devices in a mesh: groups: 4 (over y, x), seq: 16 (over z), sub: 2 (over core).
Axes of the slice: x: 2, y: 2, z: 16, core: 2. Of those that a mesh axis runs over, the one named last changes fastest.
The devices are a block of a 8x8x16 slice.
Arguments:
- query_proj: bfloat16 [8192, 4096], P(('groups', 'seq'), 'sub'), parts along dimension 0, may hold values from -2500 to 2500
- key_proj: bfloat16 [8192, 4096], P(('groups', 'seq'), 'sub'), parts along dimension 0, may hold values from -2500 to 2500
- value_proj: bfloat16 [8192, 4096], P(('groups', 'seq'), 'sub'), parts along dimension 0, may hold values from -12 to 12
- out_weight: bfloat16 [4096, 5120], P('sub', 'seq'), may hold values from -0.5 to 0.5
- query_gain: float32 [4096], P('sub'), may hold values from 0.25 to 1.75
- key_gain: float32 [4096], P('sub'), may hold values from 0.25 to 1.75
- gate_scale: float32 [20480], P(('groups', 'sub')), parts along dimension 0, may hold values from 0.5 to 2
- key_count: int32 [4], P('groups'), parts along dimension 0, may hold values from 1024 to 2048
Outputs:
- attended_out: bfloat16 [8192, 5120], P(('groups', 'seq'), 'sub'), parts along dimension 0
There are 4 independent parts, one for each index of `groups`. A program takes and returns all parts, laid end to end along the dimension named above; an argument that names none is the same for every part. Nothing has to cross between parts.
All inputs are finite; a program needn't handle non-finite values.
Results may differ from a plain program's by a relative error of at most 0.012.
Values may be sent and summed in bfloat16 or wider, within the bound.
A program may use at most 128 MiB of HBM per device.

v0:
```python
import math

import jax
import jax.numpy as jnp
from jax import lax
from jax.sharding import PartitionSpec as P

HD = 128


epsilon = 1e-06
key_block = 512


def gathered_total(array, axis):
    return lax.all_gather(array, axis).sum(0)


def cut_along(array, dim, size):
    shape = array.shape
    pieces = array.reshape(*shape[:dim], size, shape[dim] // size, *shape[dim + 1 :])
    return jnp.moveaxis(pieces, dim, 0)


def sent_and_summed(array, axis, dim):
    pieces = cut_along(array, dim, lax.axis_size(axis))
    arrived = lax.all_to_all(pieces, axis, split_axis=0, concat_axis=0, tiled=True)
    return arrived.astype(jnp.float32).sum(axis=0)


def fold_keys(running, queries, key_rows, value_rows, offset, live_keys):
    row_total = key_rows.shape[0]
    blocks = row_total // key_block
    head_count = queries.shape[1]
    key_blocks = key_rows.reshape(blocks, key_block, head_count, HD)
    value_blocks = value_rows.reshape(blocks, key_block, head_count, HD)
    scale = 1.0 / math.sqrt(HD)

    def one_block(running, element):
        key_piece, value_piece, block_index = element
        highest, weight_sum, accumulated = running
        scores = (
            jnp.einsum("qhd,khd->hqk", queries, key_piece, preferred_element_type=jnp.float32)
            * scale
        )
        positions = offset + block_index * key_block + jnp.arange(key_block)
        usable = (positions < live_keys)[None, None, :]
        scores = jnp.where(usable, scores, -1e30)
        newest = jnp.maximum(highest, jnp.max(scores, axis=2))
        shrink = jnp.exp(highest - newest)
        weights = jnp.where(usable, jnp.exp(scores - newest[:, :, None]), 0.0)
        weight_sum = weight_sum * shrink + jnp.sum(weights, axis=2)
        product = jnp.einsum(
            "hqk,khd->qhd",
            weights.astype(jnp.bfloat16),
            value_piece,
            preferred_element_type=jnp.float32,
        )
        accumulated = accumulated * shrink.T[:, :, None] + product
        return ((newest, weight_sum, accumulated), None)

    running, unused = lax.scan(one_block, running, (key_blocks, value_blocks, jnp.arange(blocks)))
    return running


def empty_state(query_rows, head_count):
    return (
        jnp.full((head_count, query_rows), -1e30, jnp.float32),
        jnp.zeros((head_count, query_rows), jnp.float32),
        jnp.zeros((query_rows, head_count, HD), jnp.float32),
    )


def finish(running):
    highest, weight_sum, accumulated = running
    result = accumulated / weight_sum.T[:, :, None]
    return result.reshape(result.shape[0], -1).astype(jnp.bfloat16)


def shards(
    query_proj, key_proj, value_proj, out_weight, query_gain, key_gain, gate_scale, key_count
):
    features = query_proj.shape[1]
    query_wide = query_proj.astype(jnp.float32)
    key_wide = key_proj.astype(jnp.float32)
    squares = (
        gathered_total(jnp.sum(query_wide * query_wide, axis=1), "sub"),
        gathered_total(jnp.sum(key_wide * key_wide, axis=1), "sub"),
    )
    all_features = features * lax.axis_size("sub")
    query_normed = (
        query_wide * lax.rsqrt(squares[0] / all_features + epsilon)[:, None] * query_gain
    ).astype(jnp.bfloat16)
    key_normed = (
        key_wide * lax.rsqrt(squares[1] / all_features + epsilon)[:, None] * key_gain
    ).astype(jnp.bfloat16)
    live_keys = key_count[0]
    query_all, key_all, value_all = (
        lax.all_to_all(query_normed, "seq", split_axis=1, concat_axis=0, tiled=True),
        lax.all_to_all(key_normed, "seq", split_axis=1, concat_axis=0, tiled=True),
        lax.all_to_all(value_proj, "seq", split_axis=1, concat_axis=0, tiled=True),
    )
    seq_rows = query_all.shape[0]
    head_count = query_all.shape[1] // HD
    running = fold_keys(
        empty_state(seq_rows, head_count),
        query_all.reshape(seq_rows, head_count, HD),
        key_all,
        value_all,
        0,
        live_keys,
    )
    attended = lax.all_to_all(finish(running), "seq", split_axis=0, concat_axis=1, tiled=True)
    partial_value = jnp.dot(
        attended,
        lax.all_gather(out_weight, "seq", axis=1, tiled=True),
        preferred_element_type=jnp.float32,
    )
    summed = sent_and_summed(partial_value.astype(jnp.bfloat16), "sub", 1)
    return (summed * gate_scale).astype(jnp.bfloat16)


def solution(mesh):
    placed = (
        P(("groups", "seq"), "sub"),
        P(("groups", "seq"), "sub"),
        P(("groups", "seq"), "sub"),
        P("sub", "seq"),
        P("sub"),
        P("sub"),
        P(("groups", "sub")),
        P("groups"),
    )
    return jax.shard_map(
        shards, mesh=mesh, in_specs=placed, out_specs=P(("groups", "seq"), "sub"), check_vma=False
    )
```

profile of v0, /device:TPU:69, one launch (start us, length us, event | category | flops | bytes accessed | tf_op | source)
XLA Modules:
  0.0 359.0 jit_solution(15972077560654113518)
XLA Ops:
  6.6 0.7 all-gather.6.cloned.1.call-update
  7.3 1.3 copy.24
  8.6 0.3 fusion.23
  8.9 11.4 %all-gather.2 = f32[2,1,128]{2,1,0:T(1,128)S(1)} all-gather(f32[1,1,128]{2,1,0:T(1,128)S(1)} %bitcast.88), channel_id=2, replica_groups=mesh['groups'=4,'seq'=16,'sub'=2] {'sub'}, dimensions={0}, use_global_device_ids=true | all-gather | bytes 1536 | tf_op jit(solution)/shard_map/all_gather | solution.py:16
  20.4 1.8 fusion.25
  22.2 8.3 %all-to-all-start = ((bf16[128,16,128]{0,2,1:T(8,128)(2,1)}), bf16[128,16,128]{0,2,1:T(8,128)(2,1)S(1)}, u32[]{:S(2)}, u32[]{:S(2)}) async-start(bf16[128,16,128]{0,2,1:T(8,128)(2,1)} %bitcast.2), calls=%async_computation | async-start | bytes 1048576 | tf_op jit(solution)/shard_map/all_to_all | solution.py:100
  30.5 0.3 copy.26
  30.8 0.3 fusion.26
  31.0 2.1 all-gather.3
  33.2 1.1 fusion.28
  34.4 26.8 %all-to-all-done = bf16[128,16,128]{0,2,1:T(8,128)(2,1)S(1)} async-done(((bf16[128,16,128]{0,2,1:T(8,128)(2,1)}), bf16[128,16,128]{0,2,1:T(8,128)(2,1)S(1)}, u32[]{:S(2)}, u32[]{:S(2)}) %all-to-all-start) | async-done | bytes 524320 | tf_op jit(solution)/shard_map/all_to_all | solution.py:100
  61.1 10.6 %all-to-all-start.1 = ((bf16[128,16,128]{0,2,1:T(8,128)(2,1)}), bf16[128,16,128]{0,2,1:T(8,128)(2,1)S(1)}, u32[]{:S(2)}, u32[]{:S(2)}) async-start(bf16[128,16,128]{0,2,1:T(8,128)(2,1)} %bitcast.7), calls=%async_computation.1 | async-start | bytes 1048576 | tf_op jit(solution)/shard_map/all_to_all | solution.py:99
  71.7 1.0 copy.28
  72.7 29.4 %all-to-all-done.1 = bf16[128,16,128]{0,2,1:T(8,128)(2,1)S(1)} async-done(((bf16[128,16,128]{0,2,1:T(8,128)(2,1)}), bf16[128,16,128]{0,2,1:T(8,128)(2,1)S(1)}, u32[]{:S(2)}, u32[]{:S(2)}) %all-to-all-start.1) | async-done | bytes 524320 | tf_op jit(solution)/shard_map/all_to_all | solution.py:99
  102.1 10.9 %all-to-all-start.2 = ((bf16[128,16,128]{0,2,1:T(8,128)(2,1)}), bf16[128,16,128]{0,2,1:T(8,128)(2,1)S(1)}, u32[]{:S(2)}, u32[]{:S(2)}) async-start(bf16[128,16,128]{0,2,1:T(8,128)(2,1)} %bitcast.10), calls=%async_computation.2 | async-start | bytes 1048576 | tf_op jit(solution)/shard_map/all_to_all | solution.py:101
  113.1 0.3 copy.25
  113.4 0.3 copy.27
  113.7 29.6 %all-to-all-done.2 = bf16[128,16,128]{0,2,1:T(8,128)(2,1)S(1)} async-done(((bf16[128,16,128]{0,2,1:T(8,128)(2,1)}), bf16[128,16,128]{0,2,1:T(8,128)(2,1)S(1)}, u32[]{:S(2)}, u32[]{:S(2)}) %all-to-all-start.2) | async-done | bytes 524320 | tf_op jit(solution)/shard_map/all_to_all | solution.py:101
  143.2 1.0 copy.29
  144.3 42.3 %while.15 = (s32[]{:T(128)}, f32[1,2048]{1,0:T(1,128)S(1)}, f32[1,2048]{1,0:T(1,128)S(1)}, f32[2048,1,128]{0,2,1:T(8,128)S(1)}, s32[4]{0:T(128)S(1)}, /*index=5*...) while((s32[]{:T(128)}, f32[1,2048]{1,0:T(1,128)S(1)}, ...), condition=%wide.region_7.8_spmd.clone, body=%wide.region_4.7_spmd.clone.sunk | while | flops 551300096 | bytes 32377536 | solution.py:62
  144.3 0.6 dynamic_slice.29
  145.5 0.7 add_compare_fusion.2
  146.2 2.7 fusion.40
  148.9 3.6 %fusion.42 = f32[2048]{0:T(1024)S(1)} fusion(f32[512,2048]{1,0:T(8,128)} %get-tuple-element.194, f32[2048]{0:T(1024)S(1)} %bitcast.74, pred[512]{0:T(512)(128)(4,1)S(1)} %add_compare_fusion.2), kind=kLoop, calls=%fused_computation.3.clone.1 | loop fusion | flops 5240832 | bytes 4211200 | tf_op jit(solution)/shard_map/while/body/eval_jaxpr/reduce_sum | solution.py:52
  152.6 2.2 fusion.44
  154.8 0.6 dynamic_slice.29
  156.1 0.7 add_compare_fusion.2
  156.7 2.7 fusion.40
  159.5 3.6 %fusion.42 = f32[2048]{0:T(1024)S(1)} fusion(f32[512,2048]{1,0:T(8,128)} %get-tuple-element.194, f32[2048]{0:T(1024)S(1)} %bitcast.74, pred[512]{0:T(512)(128)(4,1)S(1)} %add_compare_fusion.2), kind=kLoop, calls=%fused_computation.3.clone.1 | loop fusion | flops 5240832 | bytes 4211200 | tf_op jit(solution)/shard_map/while/body/eval_jaxpr/reduce_sum | solution.py:52
  163.1 2.2 fusion.44
  165.4 0.6 dynamic_slice.29
  166.6 0.7 add_compare_fusion.2
  167.3 2.7 fusion.40
  170.0 3.6 %fusion.42 = f32[2048]{0:T(1024)S(1)} fusion(f32[512,2048]{1,0:T(8,128)} %get-tuple-element.194, f32[2048]{0:T(1024)S(1)} %bitcast.74, pred[512]{0:T(512)(128)(4,1)S(1)} %add_compare_fusion.2), kind=kLoop, calls=%fused_computation.3.clone.1 | loop fusion | flops 5240832 | bytes 4211200 | tf_op jit(solution)/shard_map/while/body/eval_jaxpr/reduce_sum | solution.py:52
  173.7 2.2 fusion.44
  176.0 0.6 dynamic_slice.29
  177.2 0.7 add_compare_fusion.2
  177.9 2.7 fusion.40
  180.6 3.6 %fusion.42 = f32[2048]{0:T(1024)S(1)} fusion(f32[512,2048]{1,0:T(8,128)} %get-tuple-element.194, f32[2048]{0:T(1024)S(1)} %bitcast.74, pred[512]{0:T(512)(128)(4,1)S(1)} %add_compare_fusion.2), kind=kLoop, calls=%fused_computation.3.clone.1 | loop fusion | flops 5240832 | bytes 4211200 | tf_op jit(solution)/shard_map/while/body/eval_jaxpr/reduce_sum | solution.py:52
  184.3 2.2 fusion.44
  186.6 0.3 copy.32
  186.9 0.3 divide_convert_fusion
  187.2 41.0 %all_to_all.69 = bf16[16,128,128]{2,1,0:T(8,128)(2,1)S(1)} all-to-all(bf16[16,128,128]{2,1,0:T(8,128)(2,1)S(1)} %bitcast.78), channel_id=1, replica_groups=mesh['groups'=4,'seq'=16,'sub'=2] {'seq'}, dimensions={0} | all-to-all | bytes 1048576 | tf_op jit(solution)/shard_map/all_to_all | solution.py:113
  228.3 0.3 copy.33
  228.5 105.7 %all-gather.6.cloned.1.call-done = bf16[2048,5120]{0,1:T(8,128)(2,1)} async-done(((bf16[2048,320]{0,1:T(8,128)(2,1)}), bf16[2048,5120]{0,1:T(8,128)(2,1)}) %all-gather.6.cloned.1.call-update) | async-done | bytes 20971536 | tf_op jit(solution)/shard_map/all_gather | solution.py:116
  334.3 11.4 %convolution_convert_fusion = bf16[128,5120]{1,0:T(8,128)(2,1)S(1)} fusion(bf16[128,2048]{0,1:T(8,128)(2,1)S(1)} %bitcast.76, bf16[2048,5120]{0,1:T(8,128)(2,1)} %all-gather.6.cloned.1.call-done), kind=kOutput, calls=%fused_computation.30 | convolution fusion | flops 2685009920 | bytes 22806528 | tf_op jit(solution)/shard_map/dot_general | solution.py:114
  345.8 5.3 %all_to_all.70 = bf16[2,128,2560]{2,1,0:T(8,128)(2,1)S(1)} all-to-all(bf16[2,128,2560]{2,1,0:T(8,128)(2,1)S(1)} %bitcast.72), channel_id=1, replica_groups=mesh['groups'=4,'seq'=16,'sub'=2] {'sub'}, dimensions={0} | all-to-all | bytes 2621440 | tf_op jit(solution)/shard_map/all_to_all | solution.py:27
  351.3 0.9 multiply_convert_fusion
  (39 shorter events, 0.6 us)
Async XLA Ops:
  6.5 23.9 %copy-start.1 = (bf16[128,2048]{1,0:T(8,128)(2,1)S(1)}, bf16[128,2048]{1,0:T(8,128)(2,1)}, u32[]{:S(2)}) copy-start(bf16[128,2048]{1,0:T(8,128)(2,1)} %param.10) | copy-start | bytes 1572868
  6.5 26.7 %copy-start.4 = (f32[2048]{0:T(1024)S(1)}, f32[2048]{0:T(1024)}, u32[]{:S(2)}) copy-start(f32[2048]{0:T(1024)} %param.14) | copy-start | bytes 24580
  6.6 65.2 %copy-start.2 = (bf16[128,2048]{1,0:T(8,128)(2,1)S(1)}, bf16[128,2048]{1,0:T(8,128)(2,1)}, u32[]{:S(2)}) copy-start(bf16[128,2048]{1,0:T(8,128)(2,1)} %param.12) | copy-start | bytes 1572868
  6.6 327.7 %all-gather.6.cloned.1.call-start = ((), (), s32[]{:S(2)}) async-start(), calls=%async_computation.5 | async-start | bytes 22282240 | tf_op jit(solution)/shard_map/all_gather | solution.py:116
  22.2 39.0 %all-to-all-start = ((bf16[128,16,128]{0,2,1:T(8,128)(2,1)}), bf16[128,16,128]{0,2,1:T(8,128)(2,1)S(1)}, u32[]{:S(2)}, u32[]{:S(2)}) async-start(bf16[128,16,128]{0,2,1:T(8,128)(2,1)} %bitcast.2), calls=%async_computation | async-start | bytes 1048576 | tf_op jit(solution)/shard_map/all_to_all | solution.py:100
  61.1 41.0 %all-to-all-start.1 = ((bf16[128,16,128]{0,2,1:T(8,128)(2,1)}), bf16[128,16,128]{0,2,1:T(8,128)(2,1)S(1)}, u32[]{:S(2)}, u32[]{:S(2)}) async-start(bf16[128,16,128]{0,2,1:T(8,128)(2,1)} %bitcast.7), calls=%async_computation.1 | async-start | bytes 1048576 | tf_op jit(solution)/shard_map/all_to_all | solution.py:99
  102.1 41.1 %all-to-all-start.2 = ((bf16[128,16,128]{0,2,1:T(8,128)(2,1)}), bf16[128,16,128]{0,2,1:T(8,128)(2,1)S(1)}, u32[]{:S(2)}, u32[]{:S(2)}) async-start(bf16[128,16,128]{0,2,1:T(8,128)(2,1)} %bitcast.10), calls=%async_computation.2 | async-start | bytes 1048576 | tf_op jit(solution)/shard_map/all_to_all | solution.py:101
  148.9 3.7 %copy-start = (f32[512,2048]{1,0:T(8,128)S(1)}, f32[512,2048]{1,0:T(8,128)}, u32[]{:S(2)}) copy-start(f32[512,2048]{1,0:T(8,128)} %get-tuple-element.194) | copy-start | bytes 12582916 | tf_op jit(solution)/shard_map/while
  159.4 3.7 %copy-start = (f32[512,2048]{1,0:T(8,128)S(1)}, f32[512,2048]{1,0:T(8,128)}, u32[]{:S(2)}) copy-start(f32[512,2048]{1,0:T(8,128)} %get-tuple-element.194) | copy-start | bytes 12582916 | tf_op jit(solution)/shard_map/while
  170.0 3.7 %copy-start = (f32[512,2048]{1,0:T(8,128)S(1)}, f32[512,2048]{1,0:T(8,128)}, u32[]{:S(2)}) copy-start(f32[512,2048]{1,0:T(8,128)} %get-tuple-element.194) | copy-start | bytes 12582916 | tf_op jit(solution)/shard_map/while
  180.6 3.7 %copy-start = (f32[512,2048]{1,0:T(8,128)S(1)}, f32[512,2048]{1,0:T(8,128)}, u32[]{:S(2)}) copy-start(f32[512,2048]{1,0:T(8,128)} %get-tuple-element.194) | copy-start | bytes 12582916 | tf_op jit(solution)/shard_map/while
  345.7 5.6 %copy-start.3 = (f32[2560]{0:T(1024)S(1)}, f32[2560]{0:T(1024)}, u32[]{:S(2)}) copy-start(f32[2560]{0:T(1024)} %param.16) | copy-start | bytes 30724
Sparse Core Ops, SparseCore 0:
  9.0 325.2 all-gather.5
where the time goes:
time: 360 us; the launch traced here: 359 us
  waiting for transfers between devices  192 us (53%)
  blocking collectives  59.8 us (17%)
  matrix products  31.2 us (9%)
  starting transfers between devices  29.8 us (8%)
  other arithmetic  22.4 us (6%)
  between operations  13.6 us (4%)
  local copies, waits for them, and re-layouts  7.39 us (2%)
    all_gather x1, waiting for transfers between devices, shards(): lax.all_gather(out_weight, 'seq', axis=1, tiled=True)  106 us
    all_to_all x1, blocking collectives, shards(): lax.all_to_all(finish(running), 'seq', split_axis=0, concat_axis=1, tiled...  41 us
    all_to_all x1, waiting for transfers between devices, shards(): lax.all_to_all(value_proj, 'seq', split_axis=1, concat_axis=0, tiled=True)  29.6 us
    all_to_all x1, waiting for transfers between devices, shards(): lax.all_to_all(query_normed, 'seq', split_axis=1, concat_axis=0, tiled=True)  29.4 us
    all_to_all x1, waiting for transfers between devices, shards(): lax.all_to_all(key_normed, 'seq', split_axis=1, concat_axis=0, tiled=True)  26.8 us
    reduce_sum x4, other arithmetic, one_block(): weight_sum = weight_sum * shrink + jnp.sum(weights, axis=2)  14.5 us
    all_gather x2, blocking collectives, gathered_total(): return lax.all_gather(array, axis).sum(0)  13.5 us
    dot_general x1, matrix products, shards(): jnp.dot(attended, lax.all_gather(out_weight, 'seq', axis=1, tiled=True),...  11.4 us
  transfers between devices with their start and end apart: 4, of which 4 were waited for; matrix products, arithmetic and copies ran while one was open for 13% of the time, Pallas kernels for 0%

commit v1 on v0

v1 whole, which is shorter than its diff:
```python
import functools
import math

import jax
import jax.numpy as jnp
from jax import lax
from jax.experimental import pallas as pl
from jax.experimental.pallas import tpu as pltpu
from jax.sharding import PartitionSpec as P

HD = 128
EPSILON = 1e-06
MEMBERS = 4
CHUNK = 32
EARLY = 4
EVERY = 2
F32, BF16 = jnp.float32, jnp.bfloat16


def remote(source, target, send, arrive, where):
    return pltpu.make_async_remote_copy(
        src_ref=source,
        dst_ref=target,
        send_sem=send,
        recv_sem=arrive,
        device_id=where,
        device_id_type=pl.DeviceIdType.MESH,
    )


def nt(left, right):
    return lax.dot_general(left, right, (((1,), (1,)), ((), ())), preferred_element_type=F32)


def kernel(
    n, side, subs,
    q_in, k_in, v_in, w_in, q_gain, k_gain, gate_in, count,
    out,
    squares, squares_in, kn, qn, k_all, v_all, q_all, bias, o_out,
    att, w_half, w_all, gates, result,
    v_send, v_recv, k_send, k_recv, q_send, q_recv, o_send, o_recv,
    w_up, w_down, w_recv, small_send, small_recv, gate_send, gate_recv,
    att_send, att_recv, pair_send, pair_recv, out_send, out_recv,
):
    tokens, features = q_in.shape
    width = w_in.shape[1]
    planes = n // (MEMBERS * subs)
    columns = planes * width
    z = lax.axis_index("seq")
    s = lax.axis_index("sub")
    g = lax.axis_index("groups")
    gx, gy = g % side, g // side
    bx, by = gx % 2, gy % 2
    me = 2 * by + bx

    def square(e):
        there = g + (e % 2) * (1 - 2 * bx) + (e // 2) * side * (1 - 2 * by)
        return there, 2 * ((by + e // 2) % 2) + (bx + e) % 2

    def hop(i):
        return (i % 2) * ((i + 1) // 2) + (1 - i % 2) * ((n - i // 2) % n)

    barrier = pltpu.get_barrier_semaphore()

    def greet(i, carry):
        pl.semaphore_signal(barrier, inc=1, device_id={"seq": (z + i) % n}, device_id_type=pl.DeviceIdType.MESH)
        return carry

    lax.fori_loop(1, n, greet, 0)
    pl.semaphore_signal(barrier, inc=1, device_id={"sub": 1 - s}, device_id_type=pl.DeviceIdType.MESH)
    for e in range(1, MEMBERS):
        pl.semaphore_signal(barrier, inc=1, device_id={"groups": square(e)[0]}, device_id_type=pl.DeviceIdType.MESH)

    for index, array in enumerate((k_in, q_in)):
        total = jnp.zeros((tokens, HD), F32)
        for head in range(features // HD):
            wide = array[:, head * HD : (head + 1) * HD].astype(F32)
            total = total + wide * wide
        squares[index] = total

    pl.semaphore_wait(barrier, n - 1 + 1 + MEMBERS - 1)

    def to_peers(source, target, send, arrive):
        def one(i, carry):
            d = hop(i)
            there = (z + d) % n
            remote(source(there), target.at[pl.ds(pl.multiple_of(z * tokens, tokens), tokens), :],
                   send.at[d], arrive.at[d], {"seq": there}).start()
            return carry

        lax.fori_loop(1, n, one, 0)

    pair = remote(squares, squares_in, small_send.at[0], small_recv.at[0], {"sub": 1 - s})
    pair.start()
    to_peers(lambda there: v_in.at[:, pl.ds(pl.multiple_of(there * HD, HD), HD)], v_all, v_send, v_recv)
    gate_copies = []
    for e in range(1, MEMBERS):
        there, number = square(e)
        gate_copies.append(remote(gate_in.at[number], gates.at[me], gate_send.at[e], gate_recv.at[e], {"groups": there}))
        gate_copies[-1].start()
    gates[me] = gate_in[me]

    own = pl.ds(pl.multiple_of(z * tokens, tokens), tokens)
    pair.wait()
    for index, (array, gain, normed, full, send, arrive) in enumerate(
        ((k_in, k_gain, kn, k_all, k_send, k_recv), (q_in, q_gain, qn, q_all, q_send, q_recv))
    ):
        total = jnp.sum(squares[index] + squares_in[index], axis=1, keepdims=True)
        inverse = lax.rsqrt(total / (features * subs) + EPSILON)
        for head in range(features // HD):
            here = slice(head * HD, (head + 1) * HD)
            normed[head] = (array[:, here].astype(F32) * inverse * gain[:, here]).astype(BF16)
        to_peers(lambda there, normed=normed: normed.at[there], full, send, arrive)
        full[own, :] = normed[z]
    v_all[own, :] = v_in[:, pl.ds(pl.multiple_of(z * HD, HD), HD)]
    positions = lax.broadcasted_iota(jnp.int32, bias.shape, 1)
    bias[...] = jnp.where(positions < count[0], 0.0, -1e30)

    per_half = n // subs
    half_of, place = z // per_half, z % per_half
    gives = me == place // planes
    piece_rows = pl.ds(pl.multiple_of((place % planes) * width, 16), width)
    my_half = pl.ds(pl.multiple_of(s * features, features), features)
    weight_copy = remote(w_half, w_all.at[piece_rows, my_half], small_send.at[1], small_recv.at[1], {"sub": 1 - s})

    @pl.when(gives)
    def _():
        for head in range(features // HD):
            here = slice(head * HD, (head + 1) * HD)
            w_half[:, here] = jnp.transpose(w_in[here, :])

        @pl.when(s != half_of)
        def _():
            weight_copy.start()

        @pl.when(s == half_of)
        def _():
            def move(i, carry):
                row = pl.multiple_of((place % planes) * width + i * 16, 16)
                w_all[pl.ds(row, 16), my_half] = w_half[pl.ds(pl.multiple_of(i * 16, 16), 16), :]
                return carry

            lax.fori_loop(0, width // 16, move, 0)
            weight_copy.wait_recv()

    pieces = width // CHUNK
    events = planes * pieces
    reach = n // 2 - 1

    def ring(e):
        plane = per_half * s + planes * me + e // pieces
        k = (z - plane + n) % n
        rows = w_all.at[pl.ds(pl.multiple_of(e * CHUNK, CHUNK), CHUNK), :]
        up = remote(rows, rows, w_up.at[e], w_recv.at[e], {"seq": (z + 1) % n})
        down = remote(rows, rows, w_down.at[e], w_recv.at[e], {"seq": (z + n - 1) % n})
        return k, k < reach, (k == 0) | (k >= reach + 2), up, down

    def relay(e):
        k, goes_up, goes_down, up, down = ring(e)

        @pl.when(k != 0)
        def _():
            up.wait_recv()

        @pl.when(goes_up)
        def _():
            up.start()

        @pl.when(goes_down)
        def _():
            down.start()

    def relay_some(first, last):
        def one(e, carry):
            relay(e)
            return carry

        lax.fori_loop(first, last, one, 0)

    relay_some(0, EARLY)

    def arrived(i, carry):
        d = hop(i)
        for full, send, arrive in ((v_all, v_send, v_recv), (k_all, k_send, k_recv)):
            there = full.at[own, :]
            remote(there, there, send.at[d], arrive.at[d], {"seq": z}).wait_recv()
        return carry

    lax.fori_loop(1, n, arrived, 0)
    factor = math.log2(math.e) / math.sqrt(HD)
    mine = pl.ds(pl.multiple_of((s * MEMBERS + me) * tokens, tokens), tokens)

    def o_copy(d):
        lanes = pl.ds(pl.multiple_of(z * HD, HD), HD)
        return remote(o_out.at[d], att.at[mine, lanes], o_send.at[d], o_recv.at[d], {"seq": (z - d + n) % n})

    def attend(i, carry):
        d = hop(i)
        rows = pl.ds(pl.multiple_of(((z - d + n) % n) * tokens, tokens), tokens)

        @pl.when(i > 0)
        def _():
            there = q_all.at[own, :]
            remote(there, there, q_send.at[d], q_recv.at[d], {"seq": z}).wait_recv()

        scores = nt(q_all[rows, :], k_all[...]) * factor + bias[0:1, :]
        weights = jnp.exp2(scores - jnp.max(scores, axis=1, keepdims=True))
        denominator = jnp.sum(weights, axis=1, keepdims=True)
        summed = jnp.dot(weights.astype(BF16), v_all[...], preferred_element_type=F32)
        o_out[d] = (summed / denominator).astype(BF16)

        @pl.when(i > 0)
        def _():
            o_copy(d).start()

        @pl.when(i % EVERY == EVERY - 1)
        def _():
            relay(EARLY + i // EVERY)

        return carry

    lax.fori_loop(0, n, attend, 0)
    att[mine, pl.ds(pl.multiple_of(z * HD, HD), HD)] = o_out[0]
    done = EARLY + n // EVERY

    def o_arrived(i, carry):
        o_copy(hop(i)).wait_recv()

        @pl.when((i % 2 == 0) & (done + i // 2 <= events))
        def _():
            relay(done + i // 2 - 1)

        return carry

    lax.fori_loop(1, n, o_arrived, 0)
    done = min(events, done + (n - 1) // 2)

    def block(half, number):
        return att.at[pl.ds(pl.multiple_of((half * MEMBERS + number) * tokens, tokens), tokens), :]

    square_copies, pair_copies = {}, {}
    for e in range(1, MEMBERS):
        square_copies[e] = remote(block(s, me), block(s, me), att_send.at[e], att_recv.at[e], {"groups": square(e)[0]})
        square_copies[e].start()
    for e in range(MEMBERS):
        number = square(e)[1]
        pair_copies[e] = remote(block(s, number), block(s, number), pair_send.at[e], pair_recv.at[e], {"sub": 1 - s})
        if e:
            square_copies[e].wait_recv()
        pair_copies[e].start()
    for e in range(MEMBERS):
        pair_copies[e].wait_recv()
    for copy in gate_copies:
        copy.wait_recv()

    starts = list(range(0, columns, 256))
    out_copies = []
    for index, first in enumerate(starts):
        last = min(columns, first + 256)
        needed = -(-last // CHUNK)
        if needed > done:
            relay_some(done, needed)
            done = needed
        total = nt(att[0 : MEMBERS * tokens, :], w_all[first:last, 0:features])
        for half in range(1, subs):
            total = total + nt(
                att[half * MEMBERS * tokens : (half + 1) * MEMBERS * tokens, :],
                w_all[first:last, half * features : (half + 1) * features],
            )
        for number in range(MEMBERS):
            scaled = total[number * tokens : (number + 1) * tokens, :] * gates[number][0:1, first:last]
            result[number, :, first:last] = scaled.astype(BF16)
        lanes = pl.ds(pl.multiple_of(me * columns + first, HD), last - first)
        for e in range(1, MEMBERS):
            there, number = square(e)
            copy = remote(result.at[number, :, pl.ds(first, last - first)], out.at[:, lanes],
                          out_send.at[index, e], out_recv.at[index, e], {"groups": there})
            copy.start()
            out_copies.append(copy)
        out[:, lanes] = result[me, :, first:last]

    def sent(i, carry):
        d = hop(i)
        there = k_all.at[own, :]
        for send, arrive in ((v_send, v_recv), (k_send, k_recv), (q_send, q_recv)):
            remote(there, there, send.at[d], arrive.at[d], {"seq": z}).wait_send()
        o_copy(d).wait_send()
        return carry

    lax.fori_loop(1, n, sent, 0)

    def relayed(e, carry):
        _, goes_up, goes_down, up, down = ring(e)

        @pl.when(goes_up)
        def _():
            up.wait_send()

        @pl.when(goes_down)
        def _():
            down.wait_send()

        return carry

    lax.fori_loop(0, events, relayed, 0)

    @pl.when(gives & (s != half_of))
    def _():
        weight_copy.wait_send()

    for copy in gate_copies + list(square_copies.values()) + list(pair_copies.values()):
        copy.wait_send()
    for copy in out_copies:
        copy.wait()


def shards(n, groups, subs, q, k, v, weight, q_gain, k_gain, gate, count):
    tokens, features = q.shape
    width = weight.shape[1]
    planes = n // (MEMBERS * subs)
    columns = planes * width
    events = planes * (width // CHUNK)
    blocks = -(-columns // 256)
    gate = jnp.broadcast_to(gate.reshape(MEMBERS, 1, columns), (MEMBERS, 8, columns))
    vmem = pl.BlockSpec(memory_space=pltpu.VMEM)
    dma = pltpu.SemaphoreType.DMA
    rows = n * tokens
    return pl.pallas_call(
        functools.partial(kernel, n, math.isqrt(groups), subs),
        out_shape=jax.ShapeDtypeStruct((tokens, MEMBERS * columns), BF16),
        in_specs=[vmem] * 7 + [pl.BlockSpec(memory_space=pltpu.SMEM)],
        out_specs=vmem,
        scratch_shapes=[
            pltpu.VMEM((2, tokens, HD), F32),
            pltpu.VMEM((2, tokens, HD), F32),
            pltpu.VMEM((n, tokens, HD), BF16),
            pltpu.VMEM((n, tokens, HD), BF16),
            pltpu.VMEM((rows, HD), BF16),
            pltpu.VMEM((rows, HD), BF16),
            pltpu.VMEM((rows, HD), BF16),
            pltpu.VMEM((8, rows), F32),
            pltpu.VMEM((n, tokens, HD), BF16),
            pltpu.VMEM((subs * MEMBERS * tokens, features), BF16),
            pltpu.VMEM((width, features), BF16),
            pltpu.VMEM((columns, subs * features), BF16),
            pltpu.VMEM((MEMBERS, 8, columns), F32),
            pltpu.VMEM((MEMBERS, tokens, columns), BF16),
        ]
        + [dma((n,))] * 8
        + [dma((events,))] * 3
        + [dma((2,))] * 2
        + [dma((MEMBERS,))] * 6
        + [dma((blocks, MEMBERS))] * 2,
        compiler_params=pltpu.CompilerParams(
            collective_id=0, has_side_effects=True, vmem_limit_bytes=56 * 2**20
        ),
        name="attention",
    )(q, k, v, weight, q_gain.reshape(1, -1), k_gain.reshape(1, -1), gate, count)


def solution(mesh):
    placed = (
        P(("groups", "seq"), "sub"),
        P(("groups", "seq"), "sub"),
        P(("groups", "seq"), "sub"),
        P("sub", "seq"),
        P("sub"),
        P("sub"),
        P(("groups", "sub")),
        P("groups"),
    )
    return jax.shard_map(
        functools.partial(shards, mesh.shape["seq"], mesh.shape["groups"], mesh.shape["sub"]),
        mesh=mesh,
        in_specs=placed,
        out_specs=P(("groups", "seq"), "sub"),
        check_vma=False,
    )
```

time: 360 us -> 301 us (0.84); the launches traced: 359 us -> 296 us
  Pallas kernels: 0 us -> 290 us
  waiting for transfers between devices: 192 us -> 0 us
  blocking collectives: 59.8 us -> 0 us
  matrix products: 31.2 us -> 0 us
  starting transfers between devices: 29.8 us -> 0 us
  other arithmetic: 22.4 us -> 0 us
  between operations: 13.6 us -> 0.66 us
    pallas_call x0 -> x1, Pallas kernels: none -> 290 us  [shards(): pl.pallas_call(functools.partial(kernel, n, math.isqrt(groups), subs), ou...]
    all_gather x1 -> x0, waiting for transfers between devices: 106 us -> none  [shards(): lax.all_gather(out_weight, 'seq', axis=1, tiled=True)]
    all_to_all x3 -> x0, waiting for transfers between devices: 85.7 us -> none  [the longest x1 29.6 us: shards(): lax.all_to_all(value_proj, 'seq', split_axis=1, concat_axis=0, tiled=True)]
    all_to_all x2 -> x0, blocking collectives: 46.3 us -> none  [the longest x1 41 us: shards(): lax.all_to_all(finish(running), 'seq', split_axis=0, concat_axis=1, tiled...]
    dot_general x9 -> x0, matrix products: 31.2 us -> none  [the longest x1 11.4 us: shards(): jnp.dot(attended, lax.all_gather(out_weight, 'seq', axis=1, tiled=True),...]
    all_to_all x3 -> x0, starting transfers between devices: 29.8 us -> none  [the longest x1 10.9 us: shards(): lax.all_to_all(value_proj, 'seq', split_axis=1, concat_axis=0, tiled=True)]
    reduce_sum x9 -> x0, other arithmetic: 15.4 us -> none  [the longest x4 14.5 us: one_block(): weight_sum = weight_sum * shrink + jnp.sum(weights, axis=2)]
    all_gather x2 -> x0, blocking collectives: 13.5 us -> none  [gathered_total(): return lax.all_gather(array, axis).sum(0)]
  transfers between devices with their start and end apart: 4 -> 0, of which waited for: 4 -> 0; matrix products, arithmetic and copies ran while one was open for 13% -> 0% of each run, Pallas kernels for 0% -> 0%
where the time goes in v1:
time: 301 us; the launch traced here: 296 us
  Pallas kernels  290 us (96%)
  local copies, waits for them, and re-layouts  5.88 us (2%)
    pallas_call x1, Pallas kernels, shards(): pl.pallas_call(functools.partial(kernel, n, math.isqrt(groups), subs), ou...  290 us

profile of v1, /device:TPU:69, one launch (start us, length us, event | category | flops | bytes accessed | tf_op | source)
XLA Modules:
  0.0 296.1 jit_solution(7951866164710023086)
XLA Ops:
  0.7 0.7 broadcast_in_dim.7
  1.4 0.6 broadcast_in_dim.8.gate_in
  2.0 2.6 copy.9.w_in
  4.6 289.5 %attention.1 = bf16[128,2560]{1,0:T(8,128)(2,1)} custom-call(bf16[128,2048]{1,0:T(8,128)(2,1)} %q_in.1, bf16[128,2048]{1,0:T(8,128)(2,1)} %k_in.1, bf16[128,2048]{1,0:T(8,128)(2,1)} %v_in.1, bf16[2048,320]{1,0:T(8,128)(2,1)} %copy.9.w_in, f32[1,2048]{1,0:T(1,128)} %bitcast.2, f32[1,2048]{1,0:T(1,128)} %bitcast.3, f32[4,8,640]{2,1,0:T(8,128)} %broadcast_in_dim.8.gate_in, ...), custom_call_target="tpu_custom_call" | custom-call | tf_op jit(solution)/shard_map/attention/pallas_call | solution.py:328
  294.1 2.0 copy.12

commit v2 on v1

v2 whole, which is shorter than its diff:
```python
import functools
import math

import jax
import jax.numpy as jnp
from jax import lax
from jax.experimental import pallas as pl
from jax.experimental.pallas import tpu as pltpu
from jax.sharding import PartitionSpec as P

HD = 128
EPSILON = 1e-06
MEMBERS = 4
CUTS = (48, 32)
IN_ATTENTION = ((12, 1), (16, 2))
IN_RETURN = ((6, 3), (12, 4))
IN_SQUARE = {0: 5, 2: 6}
IN_PROJECTION = ((5, 7), (13, 8))
F32, BF16 = jnp.float32, jnp.bfloat16


def remote(source, target, send, arrive, where):
    return pltpu.make_async_remote_copy(
        src_ref=source,
        dst_ref=target,
        send_sem=send,
        recv_sem=arrive,
        device_id=where,
        device_id_type=pl.DeviceIdType.MESH,
    )


def nt(left, right):
    return lax.dot_general(left, right, (((1,), (1,)), ((), ())), preferred_element_type=F32)


def kernel(
    n, side, subs,
    q_any, k_any, v_any, w_any, q_gain, k_gain, gate_in, count,
    out,
    q_in, k_in, v_in, gate_turned, squares, squares_in, kn, qn, k_all, v_all, q_all, bias, o_out,
    att, w_ring, w_pair, gates, result,
    load, v_send, v_recv, k_send, k_recv, q_send, q_recv, o_send, o_recv,
    ring_send, ring_recv, w_send, w_recv, small_send, small_recv, gate_send, gate_recv,
    att_send, att_recv, pair_send, pair_recv, out_send, out_recv,
):
    tokens, features = q_in.shape
    share = w_any.shape[0] // MEMBERS
    per_half = n // subs
    z = lax.axis_index("seq")
    s = lax.axis_index("sub")
    g = lax.axis_index("groups")
    gx, gy = g % side, g // side
    bx, by = gx % 2, gy % 2
    me = 2 * by + bx

    def square(e):
        there = g + (e % 2) * (1 - 2 * bx) + (e // 2) * side * (1 - 2 * by)
        return there, 2 * ((by + e // 2) % 2) + (bx + e) % 2

    def hop(i):
        return (i % 2) * ((i + 1) // 2) + (1 - i % 2) * ((n - i // 2) % n)

    barrier = pltpu.get_barrier_semaphore()

    def greet(i, carry):
        pl.semaphore_signal(barrier, inc=1, device_id={"seq": (z + i) % n}, device_id_type=pl.DeviceIdType.MESH)
        return carry

    lax.fori_loop(1, n, greet, 0)
    pl.semaphore_signal(barrier, inc=1, device_id={"sub": 1 - s}, device_id_type=pl.DeviceIdType.MESH)
    for e in range(1, MEMBERS):
        pl.semaphore_signal(barrier, inc=1, device_id={"groups": square(e)[0]}, device_id_type=pl.DeviceIdType.MESH)

    loads = [
        pltpu.make_async_copy(source, target, load.at[index])
        for index, (source, target) in enumerate(((k_any, k_in), (q_any, q_in), (v_any, v_in)))
    ]
    for copy in loads:
        copy.start()

    for index, array in enumerate((k_in, q_in)):
        loads[index].wait()
        total = jnp.zeros((tokens, HD), F32)
        for head in range(features // HD):
            wide = array[:, head * HD : (head + 1) * HD].astype(F32)
            total = total + wide * wide
        squares[index] = total

    weight_load = pltpu.make_async_copy(
        w_any.at[pl.ds(pl.multiple_of(me * share, 16), share), :],
        w_ring.at[pl.ds(pl.multiple_of(z * share, 16), share), :],
        load.at[3],
    )
    weight_load.start()

    gate = gate_in[...].reshape(1, gate_in.shape[0])
    for first in range(0, gate_in.shape[0], HD):
        gate_turned[first : first + HD, :] = jnp.transpose(jnp.broadcast_to(gate[:, first : first + HD], (HD, HD)))
    loads[2].wait()
    with jax.named_scope("barrier"):
        pl.semaphore_wait(barrier, n - 1 + 1 + MEMBERS - 1)

    pair = remote(squares, squares_in, small_send.at[0], small_recv.at[0], {"sub": 1 - s})
    pair.start()

    own = pl.ds(pl.multiple_of(z * tokens, tokens), tokens)

    def v_block(there):
        return v_in.at[:, pl.ds(pl.multiple_of(there * HD, HD), HD)]

    exchanges = (
        (v_block, v_all, v_send, v_recv),
        (lambda there: kn.at[there], k_all, k_send, k_recv),
        (lambda there: qn.at[there], q_all, q_send, q_recv),
    )

    def to_peers(array, first, last):
        source, target, send, arrive = exchanges[array]

        def one(i, carry):
            d = hop(i)
            there = (z + d) % n
            remote(source(there), target.at[own, :], send.at[d], arrive.at[d], {"seq": there}).start()
            return carry

        lax.fori_loop(first, last, one, 0)

    to_peers(0, 1, n)

    def gate_rows(i, number):
        return pl.ds(pl.multiple_of((i * MEMBERS + number) * share, 16), share)

    def gate_copy(i, e):
        there, number = square(e)
        return remote(gate_turned.at[gate_rows(i, number), :],
                      gates.at[pl.ds(pl.multiple_of((me * per_half + i) * share, 16), share), :],
                      gate_send.at[i, e], gate_recv.at[i, e], {"groups": there})

    def gate_out(i, carry):
        for e in range(1, MEMBERS):
            gate_copy(i, e).start()
        gates[pl.ds(pl.multiple_of((me * per_half + i) * share, 16), share), :] = gate_turned[gate_rows(i, me), :]
        return carry

    lax.fori_loop(0, per_half, gate_out, 0)

    pair.wait()
    for index, (array, gain, normed, full) in enumerate(((k_in, k_gain, kn, k_all), (q_in, q_gain, qn, q_all))):
        total = jnp.sum(squares[index] + squares_in[index], axis=1, keepdims=True)
        inverse = lax.rsqrt(total / (features * subs) + EPSILON)
        for head in range(features // HD):
            here = slice(head * HD, (head + 1) * HD)
            normed[head] = (array[:, here].astype(F32) * inverse * gain[:, here]).astype(BF16)
        to_peers(1 + index, 1, n)
        full[own, :] = normed[z]
    v_all[own, :] = v_in[:, pl.ds(pl.multiple_of(z * HD, HD), HD)]
    positions = lax.broadcasted_iota(jnp.int32, bias.shape, 1)
    bias[...] = jnp.where(positions < count[0], 0.0, -1e30)

    weight_load.wait()

    def ring(k, upwards, chunk):
        plane = (z - k + n) % n if upwards else (z + k) % n
        start = plane * share + sum(CUTS[:chunk])
        rows = w_ring.at[pl.ds(pl.multiple_of(start, 16), CUTS[chunk]), :]
        to = (z + 1) % n if upwards else (z + n - 1) % n
        lane = 2 * chunk + upwards
        send, arrive = ring_send.at[lane, k], ring_recv.at[lane, k]
        return remote(rows, rows, send, arrive, {"seq": to})

    ways = [(upwards, chunk, n // 2 - (upwards != (chunk == 0))) for chunk in (0, 1) for upwards in (True, False)]

    def pair_weights(plane):
        row = pl.multiple_of((plane % per_half) * share, 16)
        return remote(w_ring.at[pl.ds(pl.multiple_of(plane * share, 16), share), :], w_pair.at[pl.ds(row, share), :],
                      w_send.at[plane % per_half], w_recv.at[plane % per_half], {"sub": 1 - s})

    def have(plane):
        @pl.when(plane // per_half != s)
        def _():
            pair_weights(plane).start()

    def relay(k):
        if k:
            with jax.named_scope(f"relay{k}"):
                for upwards, chunk, hops in ways:
                    if k <= hops:
                        ring_arrival(k, upwards, chunk).wait_recv()
                    if k < hops:
                        ring(k, upwards, chunk).start()
            have((z + k) % n)
            if 2 * k < n:
                have((z - k + n) % n)
        else:
            for upwards, chunk, hops in ways:
                ring(0, upwards, chunk).start()
            have(z)

    def ring_arrival(k, upwards, chunk):
        plane = (z - k + n) % n if upwards else (z + k) % n
        start = plane * share + sum(CUTS[:chunk])
        rows = w_ring.at[pl.ds(pl.multiple_of(start, 16), CUTS[chunk]), :]
        lane = 2 * chunk + upwards
        return remote(rows, rows, ring_send.at[lane, k - 1], ring_recv.at[lane, k - 1], {"seq": z})

    relay(0)

    def arrived(i, carry):
        d = hop(i)
        for full, send, arrive in ((v_all, v_send, v_recv), (k_all, k_send, k_recv)):
            there = full.at[own, :]
            remote(there, there, send.at[d], arrive.at[d], {"seq": z}).wait_recv()
        return carry

    with jax.named_scope("vk"):
        lax.fori_loop(1, n, arrived, 0)
    factor = math.log2(math.e) / math.sqrt(HD)
    mine = pl.ds(pl.multiple_of((s * MEMBERS + me) * tokens, tokens), tokens)

    def o_copy(d):
        lanes = pl.ds(pl.multiple_of(z * HD, HD), HD)
        return remote(o_out.at[d], att.at[mine, lanes], o_send.at[d], o_recv.at[d], {"seq": (z - d + n) % n})

    def attend(i, carry):
        d = hop(i)
        rows = pl.ds(pl.multiple_of(((z - d + n) % n) * tokens, tokens), tokens)

        @pl.when(i > 0)
        def _():
            there = q_all.at[own, :]
            with jax.named_scope("q"):
                remote(there, there, q_send.at[d], q_recv.at[d], {"seq": z}).wait_recv()

        scores = nt(q_all[rows, :], k_all[...]) * factor + bias[0:1, :]
        weights = jnp.exp2(scores - jnp.max(scores, axis=1, keepdims=True))
        denominator = jnp.sum(weights, axis=1, keepdims=True)
        summed = jnp.dot(weights.astype(BF16), v_all[...], preferred_element_type=F32)
        o_out[d] = (summed / denominator).astype(BF16)

        @pl.when(i > 0)
        def _():
            o_copy(d).start()

        return carry

    def spread(body, first, last, points):
        for stop, k in points:
            lax.fori_loop(first, stop, body, 0)
            relay(k)
            first = stop
        lax.fori_loop(first, last, body, 0)

    with jax.named_scope("attend"):
        spread(attend, 0, n, IN_ATTENTION)
    att[mine, pl.ds(pl.multiple_of(z * HD, HD), HD)] = o_out[0]

    def o_arrived(i, carry):
        o_copy(hop(i)).wait_recv()
        return carry

    with jax.named_scope("o"):
        spread(o_arrived, 1, n, IN_RETURN)

    def block(half, number):
        return att.at[pl.ds(pl.multiple_of((half * MEMBERS + number) * tokens, tokens), tokens), :]

    square_copies, pair_copies = {}, {}
    for e in range(1, MEMBERS):
        square_copies[e] = remote(block(s, me), block(s, me), att_send.at[e], att_recv.at[e], {"groups": square(e)[0]})
        square_copies[e].start()
    for e in range(MEMBERS):
        number = square(e)[1]
        pair_copies[e] = remote(block(s, number), block(s, number), pair_send.at[e], pair_recv.at[e], {"sub": 1 - s})
        if e:
            with jax.named_scope(f"square{e}"):
                square_copies[e].wait_recv()
        pair_copies[e].start()
        if e in IN_SQUARE:
            relay(IN_SQUARE[e])
    for e in range(MEMBERS):
        with jax.named_scope(f"pair{e}"):
            pair_copies[e].wait_recv()

    def gates_arrived(i, carry):
        for e in range(1, MEMBERS):
            gate_copy(i, e).wait_recv()
        return carry

    lax.fori_loop(0, per_half, gates_arrived, 0)

    every = MEMBERS * tokens

    def half_att(half):
        return att[pl.ds(pl.multiple_of(half * every, HD), every), :]

    def out_copy(i, e):
        there, number = square(e)
        return remote(result.at[pl.ds(pl.multiple_of((number * per_half + i) * share, 16), share), :],
                      out.at[gate_rows(i, me), :], out_send.at[i, e], out_recv.at[i, e], {"groups": there})

    def project(j, carry):
        plane = (z + hop(j)) % n
        i = plane % per_half

        @pl.when(plane // per_half == s)
        def _():
            with jax.named_scope("pairw"):
                pair_weights(plane).wait_recv()
            with jax.named_scope("project"):
                total = nt(w_ring[pl.ds(pl.multiple_of(plane * share, 16), share), :], half_att(s))
                total = total + nt(w_pair[pl.ds(pl.multiple_of(i * share, 16), share), :], half_att(1 - s))
                for number in range(MEMBERS):
                    rows = pl.ds(pl.multiple_of((number * per_half + i) * share, 16), share)
                    result[rows, :] = (total[:, number * tokens : (number + 1) * tokens] * gates[rows, :]).astype(BF16)
            for e in range(1, MEMBERS):
                out_copy(i, e).start()
            out[gate_rows(i, me), :] = result[pl.ds(pl.multiple_of((me * per_half + i) * share, 16), share), :]

        return carry

    spread(project, 0, n, IN_PROJECTION)

    def sent(i, carry):
        d = hop(i)
        there = k_all.at[own, :]
        for send, arrive in ((v_send, v_recv), (k_send, k_recv), (q_send, q_recv)):
            remote(there, there, send.at[d], arrive.at[d], {"seq": z}).wait_send()
        o_copy(d).wait_send()
        return carry

    lax.fori_loop(1, n, sent, 0)

    for upwards, chunk, hops in ways:
        for k in range(hops):
            ring(k, upwards, chunk).wait_send()

    def finished(i, carry):
        pair_weights((1 - s) * per_half + i).wait_send()
        for e in range(1, MEMBERS):
            gate_copy(i, e).wait_send()
            out_copy(i, e).wait()
        return carry

    for copy in list(square_copies.values()) + list(pair_copies.values()):
        copy.wait_send()
    with jax.named_scope("out"):
        lax.fori_loop(0, per_half, finished, 0)


def shards(n, groups, subs, q, k, v, weight, q_gain, k_gain, gate, count):
    tokens, features = q.shape
    width = weight.shape[1]
    share, per_half = width // MEMBERS, n // subs
    vmem = pl.BlockSpec(memory_space=pltpu.VMEM)
    hbm = pl.BlockSpec(memory_space=pl.ANY)
    dma = pltpu.SemaphoreType.DMA
    rows = n * tokens
    return pl.pallas_call(
        functools.partial(kernel, n, math.isqrt(groups), subs),
        out_shape=jax.ShapeDtypeStruct((per_half * width, tokens), BF16),
        in_specs=[hbm] * 4 + [vmem] * 3 + [pl.BlockSpec(memory_space=pltpu.SMEM)],
        out_specs=vmem,
        scratch_shapes=[
            pltpu.VMEM((tokens, features), BF16),
            pltpu.VMEM((tokens, features), BF16),
            pltpu.VMEM((tokens, features), BF16),
            pltpu.VMEM((per_half * width, HD), F32),
            pltpu.VMEM((2, tokens, HD), F32),
            pltpu.VMEM((2, tokens, HD), F32),
            pltpu.VMEM((n, tokens, HD), BF16),
            pltpu.VMEM((n, tokens, HD), BF16),
            pltpu.VMEM((rows, HD), BF16),
            pltpu.VMEM((rows, HD), BF16),
            pltpu.VMEM((rows, HD), BF16),
            pltpu.VMEM((8, rows), F32),
            pltpu.VMEM((n, tokens, HD), BF16),
            pltpu.VMEM((subs * MEMBERS * tokens, features), BF16),
            pltpu.VMEM((n * share, features), BF16),
            pltpu.VMEM((per_half * share, features), BF16),
            pltpu.VMEM((MEMBERS * per_half * share, HD), F32),
            pltpu.VMEM((MEMBERS * per_half * share, tokens), BF16),
            dma((4,)),
        ]
        + [dma((n,))] * 8
        + [dma((4, n // 2))] * 2
        + [dma((per_half,))] * 2
        + [dma((1,))] * 2
        + [dma((per_half, MEMBERS))] * 2
        + [dma((MEMBERS,))] * 4
        + [dma((per_half, MEMBERS))] * 2,
        compiler_params=pltpu.CompilerParams(
            collective_id=0, has_side_effects=True, vmem_limit_bytes=56 * 2**20
        ),
        name="attention",
    )(q, k, v, weight.T, q_gain.reshape(1, -1), k_gain.reshape(1, -1), gate, count).T


def solution(mesh):
    placed = (
        P(("groups", "seq"), "sub"),
        P(("groups", "seq"), "sub"),
        P(("groups", "seq"), "sub"),
        P("sub", "seq"),
        P("sub"),
        P("sub"),
        P(("groups", "sub")),
        P("groups"),
    )
    return jax.shard_map(
        functools.partial(shards, mesh.shape["seq"], mesh.shape["groups"], mesh.shape["sub"]),
        mesh=mesh,
        in_specs=placed,
        out_specs=P(("groups", "seq"), "sub"),
        check_vma=False,
    )
```

time: 301 us -> 187 us (0.62); the launches traced: 296 us -> 187 us
  Pallas kernels: 290 us -> 184 us
  local copies, waits for them, and re-layouts: 5.88 us -> 2.16 us
    pallas_call x1, Pallas kernels: 290 us -> 184 us  [shards(): pl.pallas_call(functools.partial(kernel, n, math.isqrt(groups), subs), ou...]
    unnamed x2 -> x0, local copies, waits for them, and re-layouts: 4.52 us -> none
where the time goes in v2:
time: 187 us
  Pallas kernels  184 us (98%)
  local copies, waits for them, and re-layouts  2.16 us (1%)
    pallas_call x1, Pallas kernels, shards(): pl.pallas_call(functools.partial(kernel, n, math.isqrt(groups), subs), ou...  184 us

profile of v2, /device:TPU:69, one launch (start us, length us, event | category | flops | bytes accessed | tf_op | source)
XLA Modules:
  0.0 186.8 jit_solution(15465779659374365383)
XLA Ops:
  0.7 184.0 %attention.1 = bf16[2560,128]{1,0:T(8,128)(2,1)} custom-call(bf16[128,2048]{1,0:T(8,128)(2,1)} %q_any.1, bf16[128,2048]{1,0:T(8,128)(2,1)} %k_any.1, bf16[128,2048]{1,0:T(8,128)(2,1)} %v_any.1, bf16[320,2048]{1,0:T(8,128)(2,1)} %bitcast.5, f32[1,2048]{1,0:T(1,128)} %bitcast.6, f32[1,2048]{1,0:T(1,128)} %bitcast.7, f32[2560]{0:T(1024)} %gate_in.1, ...), custom_call_target="tpu_custom_call" | custom-call | tf_op jit(solution)/shard_map/attention/pallas_call | solution.py:359
  184.6 2.2 %copy.9 = bf16[128,2560]{1,0:T(8,128)(2,1)} copy(bf16[128,2560]{0,1:T(8,128)(2,1)} %bitcast.4) | data formatting | bytes 1310720 | tf_op jit(solution)/shard_map/transpose | solution.py:396

commit v3 on v2

--- a/solution.py
+++ b/solution.py
@@ -12,10 +12,9 @@
 EPSILON = 1e-06
 MEMBERS = 4
 CUTS = (48, 32)
-IN_ATTENTION = ((12, 1), (16, 2))
-IN_RETURN = ((6, 3), (12, 4))
-IN_SQUARE = {0: 5, 2: 6}
-IN_PROJECTION = ((5, 7), (13, 8))
+IN_ATTENTION = ((6, 0), (16, 1))
+IN_SQUARE = {0: 2}
+IN_PROJECTION = ((5, 3), (7, 4), (9, 5), (11, 6), (13, 7), (15, 8))
 F32, BF16 = jnp.float32, jnp.bfloat16
 
 
@@ -36,13 +35,12 @@
 
 def kernel(
     n, side, subs,
-    q_any, k_any, v_any, w_any, q_gain, k_gain, gate_in, count,
+    q_any, k_any, v_any, w_any, q_gain_any, k_gain_any, gate_any, count,
     out,
-    q_in, k_in, v_in, gate_turned, squares, squares_in, kn, qn, k_all, v_all, q_all, bias, o_out,
+    q_in, k_in, v_in, q_gain, k_gain, gate_in, gate_turned, squares, squares_in, kn, qn, k_all, v_all, q_all, bias, o_out,
     att, w_ring, w_pair, gates, result,
-    load, v_send, v_recv, k_send, k_recv, q_send, q_recv, o_send, o_recv,
-    ring_send, ring_recv, w_send, w_recv, small_send, small_recv, gate_send, gate_recv,
-    att_send, att_recv, pair_send, pair_recv, out_send, out_recv,
+    load, sends, v_recv, k_recv, q_recv, o_recv,
+    ring_recv, w_recv, small_recv, gate_recv, att_recv, pair_recv, out_recv, out_own,
 ):
     tokens, features = q_in.shape
     share = w_any.shape[0] // MEMBERS
@@ -64,7 +62,7 @@
     barrier = pltpu.get_barrier_semaphore()
 
     def greet(i, carry):
-        pl.semaphore_signal(barrier, inc=1, device_id={"seq": (z + i) % n}, device_id_type=pl.DeviceIdType.MESH)
+        pl.semaphore_signal(barrier, inc=1, device_id={"seq": (z + hop(n - i)) % n}, device_id_type=pl.DeviceIdType.MESH)
         return carry
 
     lax.fori_loop(1, n, greet, 0)
@@ -74,7 +72,9 @@
 
     loads = [
         pltpu.make_async_copy(source, target, load.at[index])
-        for index, (source, target) in enumerate(((k_any, k_in), (q_any, q_in), (v_any, v_in)))
+        for index, (source, target) in enumerate((
+            (k_any, k_in), (q_any, q_in), (v_any, v_in), (k_gain_any, k_gain), (q_gain_any, q_gain), (gate_any, gate_in),
+        ))
     ]
     for copy in loads:
         copy.start()
@@ -90,44 +90,45 @@
     weight_load = pltpu.make_async_copy(
         w_any.at[pl.ds(pl.multiple_of(me * share, 16), share), :],
         w_ring.at[pl.ds(pl.multiple_of(z * share, 16), share), :],
-        load.at[3],
+        load.at[6],
     )
     weight_load.start()
 
+    loads[2].wait()
+    with jax.named_scope("barrier"):
+        pl.semaphore_wait(barrier, n - 1 + 1 + MEMBERS - 1)
+
+    pair = remote(squares, squares_in, sends.at[1], small_recv.at[0], {"sub": 1 - s})
+    pair.start()
+
+    own = pl.ds(pl.multiple_of(z * tokens, tokens), tokens)
+
+    def v_block(there):
+        return v_in.at[:, pl.ds(pl.multiple_of(there * HD, HD), HD)]
+
+    exchanges = (
+        (v_block, v_all, lambda d: v_recv.at[0]),
+        (lambda there: kn.at[there], k_all, lambda d: k_recv.at[0]),
+        (lambda there: qn.at[there], q_all, lambda d: q_recv.at[d]),
+    )
+
+    def to_peers(array, first, last):
+        source, target, arrive = exchanges[array]
+
+        def one(i, carry):
+            d = hop(i)
+            there = (z + d) % n
+            remote(source(there), target.at[own, :], sends.at[0], arrive(d), {"seq": there}).start()
+            return carry
+
+        lax.fori_loop(first, last, one, 0)
+
+    to_peers(0, 1, n)
+
+    loads[5].wait()
     gate = gate_in[...].reshape(1, gate_in.shape[0])
     for first in range(0, gate_in.shape[0], HD):
         gate_turned[first : first + HD, :] = jnp.transpose(jnp.broadcast_to(gate[:, first : first + HD], (HD, HD)))
-    loads[2].wait()
-    with jax.named_scope("barrier"):
-        pl.semaphore_wait(barrier, n - 1 + 1 + MEMBERS - 1)
-
-    pair = remote(squares, squares_in, small_send.at[0], small_recv.at[0], {"sub": 1 - s})
-    pair.start()
-
-    own = pl.ds(pl.multiple_of(z * tokens, tokens), tokens)
-
-    def v_block(there):
-        return v_in.at[:, pl.ds(pl.multiple_of(there * HD, HD), HD)]
-
-    exchanges = (
-        (v_block, v_all, v_send, v_recv),
-        (lambda there: kn.at[there], k_all, k_send, k_recv),
-        (lambda there: qn.at[there], q_all, q_send, q_recv),
-    )
-
-    def to_peers(array, first, last):
-        source, target, send, arrive = exchanges[array]
-
-        def one(i, carry):
-            d = hop(i)
-            there = (z + d) % n
-            remote(source(there), target.at[own, :], send.at[d], arrive.at[d], {"seq": there}).start()
-            return carry
-
-        lax.fori_loop(first, last, one, 0)
-
-    to_peers(0, 1, n)
-
     def gate_rows(i, number):
         return pl.ds(pl.multiple_of((i * MEMBERS + number) * share, 16), share)
 
@@ -135,7 +136,7 @@
         there, number = square(e)
         return remote(gate_turned.at[gate_rows(i, number), :],
                       gates.at[pl.ds(pl.multiple_of((me * per_half + i) * share, 16), share), :],
-                      gate_send.at[i, e], gate_recv.at[i, e], {"groups": there})
+                      sends.at[2], gate_recv.at[0], {"groups": there})
 
     def gate_out(i, carry):
         for e in range(1, MEMBERS):
@@ -145,7 +146,9 @@
 
     lax.fori_loop(0, per_half, gate_out, 0)
 
-    pair.wait()
+    pair.wait_recv()
+    loads[3].wait()
+    loads[4].wait()
     for index, (array, gain, normed, full) in enumerate(((k_in, k_gain, kn, k_all), (q_in, q_gain, qn, q_all))):
         total = jnp.sum(squares[index] + squares_in[index], axis=1, keepdims=True)
         inverse = lax.rsqrt(total / (features * subs) + EPSILON)
@@ -166,15 +169,14 @@
         rows = w_ring.at[pl.ds(pl.multiple_of(start, 16), CUTS[chunk]), :]
         to = (z + 1) % n if upwards else (z + n - 1) % n
         lane = 2 * chunk + upwards
-        send, arrive = ring_send.at[lane, k], ring_recv.at[lane, k]
-        return remote(rows, rows, send, arrive, {"seq": to})
+        return remote(rows, rows, sends.at[3], ring_recv.at[lane, k], {"seq": to})
 
     ways = [(upwards, chunk, n // 2 - (upwards != (chunk == 0))) for chunk in (0, 1) for upwards in (True, False)]
 
     def pair_weights(plane):
         row = pl.multiple_of((plane % per_half) * share, 16)
         return remote(w_ring.at[pl.ds(pl.multiple_of(plane * share, 16), share), :], w_pair.at[pl.ds(row, share), :],
-                      w_send.at[plane % per_half], w_recv.at[plane % per_half], {"sub": 1 - s})
+                      sends.at[4], w_recv.at[plane % per_half], {"sub": 1 - s})
 
     def have(plane):
         @pl.when(plane // per_half != s)
@@ -202,25 +204,21 @@
         start = plane * share + sum(CUTS[:chunk])
         rows = w_ring.at[pl.ds(pl.multiple_of(start, 16), CUTS[chunk]), :]
         lane = 2 * chunk + upwards
-        return remote(rows, rows, ring_send.at[lane, k - 1], ring_recv.at[lane, k - 1], {"seq": z})
-
-    relay(0)
-
-    def arrived(i, carry):
-        d = hop(i)
-        for full, send, arrive in ((v_all, v_send, v_recv), (k_all, k_send, k_recv)):
-            there = full.at[own, :]
-            remote(there, there, send.at[d], arrive.at[d], {"seq": z}).wait_recv()
-        return carry
+        return remote(rows, rows, sends.at[3], ring_recv.at[lane, k - 1], {"seq": z})
+
+    def whole(array, arrive):
+        there = array.at[pl.ds(0, (n - 1) * tokens), :]
+        return remote(there, there, sends.at[0], arrive.at[0], {"seq": z})
 
     with jax.named_scope("vk"):
-        lax.fori_loop(1, n, arrived, 0)
+        whole(v_all, v_recv).wait_recv()
+        whole(k_all, k_recv).wait_recv()
     factor = math.log2(math.e) / math.sqrt(HD)
     mine = pl.ds(pl.multiple_of((s * MEMBERS + me) * tokens, tokens), tokens)
 
     def o_copy(d):
         lanes = pl.ds(pl.multiple_of(z * HD, HD), HD)
-        return remote(o_out.at[d], att.at[mine, lanes], o_send.at[d], o_recv.at[d], {"seq": (z - d + n) % n})
+        return remote(o_out.at[d], att.at[mine, lanes], sends.at[0], o_recv.at[d], {"seq": (z - d + n) % n})
 
     def attend(i, carry):
         d = hop(i)
@@ -230,7 +228,7 @@
         def _():
             there = q_all.at[own, :]
             with jax.named_scope("q"):
-                remote(there, there, q_send.at[d], q_recv.at[d], {"seq": z}).wait_recv()
+                remote(there, there, sends.at[0], q_recv.at[d], {"seq": z}).wait_recv()
 
         scores = nt(q_all[rows, :], k_all[...]) * factor + bias[0:1, :]
         weights = jnp.exp2(scores - jnp.max(scores, axis=1, keepdims=True))
@@ -255,26 +253,34 @@
         spread(attend, 0, n, IN_ATTENTION)
     att[mine, pl.ds(pl.multiple_of(z * HD, HD), HD)] = o_out[0]
 
+    def square_copy(d, e):
+        lanes = pl.ds(pl.multiple_of(((z + d) % n) * HD, HD), HD)
+        return remote(att.at[mine, lanes], att.at[mine, lanes], sends.at[5], att_recv.at[e], {"groups": square(e)[0]})
+
     def o_arrived(i, carry):
-        o_copy(hop(i)).wait_recv()
+        d = hop(i)
+
+        @pl.when(i > 0)
+        def _():
+            o_copy(d).wait_recv()
+
+        for e in range(1, MEMBERS):
+            square_copy(d, e).start()
         return carry
 
     with jax.named_scope("o"):
-        spread(o_arrived, 1, n, IN_RETURN)
+        lax.fori_loop(0, n, o_arrived, 0)
 
     def block(half, number):
         return att.at[pl.ds(pl.multiple_of((half * MEMBERS + number) * tokens, tokens), tokens), :]
 
-    square_copies, pair_copies = {}, {}
-    for e in range(1, MEMBERS):
-        square_copies[e] = remote(block(s, me), block(s, me), att_send.at[e], att_recv.at[e], {"groups": square(e)[0]})
-        square_copies[e].start()
+    pair_copies = {}
     for e in range(MEMBERS):
         number = square(e)[1]
-        pair_copies[e] = remote(block(s, number), block(s, number), pair_send.at[e], pair_recv.at[e], {"sub": 1 - s})
+        pair_copies[e] = remote(block(s, number), block(s, number), sends.at[6], pair_recv.at[e], {"sub": 1 - s})
         if e:
             with jax.named_scope(f"square{e}"):
-                square_copies[e].wait_recv()
+                remote(block(s, number), block(s, number), sends.at[5], att_recv.at[e], {"sub": s}).wait_recv()
         pair_copies[e].start()
         if e in IN_SQUARE:
             relay(IN_SQUARE[e])
@@ -282,12 +288,13 @@
         with jax.named_scope(f"pair{e}"):
             pair_copies[e].wait_recv()
 
-    def gates_arrived(i, carry):
-        for e in range(1, MEMBERS):
-            gate_copy(i, e).wait_recv()
-        return carry
-
-    lax.fori_loop(0, per_half, gates_arrived, 0)
+    others = (MEMBERS - 1) * per_half * share
+
+    def all_gates():
+        there = gates.at[pl.ds(0, others), :]
+        return remote(there, there, sends.at[2], gate_recv.at[0], {"seq": z})
+
+    all_gates().wait_recv()
 
     every = MEMBERS * tokens
 
@@ -297,7 +304,11 @@
     def out_copy(i, e):
         there, number = square(e)
         return remote(result.at[pl.ds(pl.multiple_of((number * per_half + i) * share, 16), share), :],
-                      out.at[gate_rows(i, me), :], out_send.at[i, e], out_recv.at[i, e], {"groups": there})
+                      out.at[gate_rows(i, me), :], sends.at[7], out_recv.at[0], {"groups": there})
+
+    def own_out(i):
+        rows = pl.ds(pl.multiple_of((me * per_half + i) * share, 16), share)
+        return pltpu.make_async_copy(result.at[rows, :], out.at[gate_rows(i, me), :], out_own.at[0])
 
     def project(j, carry):
         plane = (z + hop(j)) % n
@@ -315,56 +326,51 @@
                     result[rows, :] = (total[:, number * tokens : (number + 1) * tokens] * gates[rows, :]).astype(BF16)
             for e in range(1, MEMBERS):
                 out_copy(i, e).start()
-            out[gate_rows(i, me), :] = result[pl.ds(pl.multiple_of((me * per_half + i) * share, 16), share), :]
+            own_out(i).start()
 
         return carry
 
     spread(project, 0, n, IN_PROJECTION)
 
-    def sent(i, carry):
-        d = hop(i)
-        there = k_all.at[own, :]
-        for send, arrive in ((v_send, v_recv), (k_send, k_recv), (q_send, q_recv)):
-            remote(there, there, send.at[d], arrive.at[d], {"seq": z}).wait_send()
-        o_copy(d).wait_send()
-        return carry
-
-    lax.fori_loop(1, n, sent, 0)
-
-    for upwards, chunk, hops in ways:
-        for k in range(hops):
-            ring(k, upwards, chunk).wait_send()
-
-    def finished(i, carry):
-        pair_weights((1 - s) * per_half + i).wait_send()
-        for e in range(1, MEMBERS):
-            gate_copy(i, e).wait_send()
-            out_copy(i, e).wait()
-        return carry
-
-    for copy in list(square_copies.values()) + list(pair_copies.values()):
-        copy.wait_send()
+    def all_sent(array, rows, index):
+        there = array.at[pl.ds(0, rows), :]
+        remote(there, there, sends.at[index], small_recv.at[0], {"seq": z}).wait_send()
+
+    peers = (n - 1) * tokens * HD // features
+    all_sent(att, 4 * peers, 0)
+    pair.wait_send()
+    all_gates().wait_send()
+    all_sent(w_ring, (n - 1) * share, 3)
+    all_sent(w_pair, per_half * share, 4)
+    all_sent(att, (MEMBERS - 1) * tokens, 5)
+    all_sent(att, MEMBERS * tokens, 6)
+    all_sent(result, others, 7)
     with jax.named_scope("out"):
-        lax.fori_loop(0, per_half, finished, 0)
+        there = out.at[pl.ds(0, others), :]
+        remote(there, there, sends.at[7], out_recv.at[0], {"seq": z}).wait_recv()
+        mine_out = out.at[pl.ds(0, per_half * share), :]
+        pltpu.make_async_copy(result.at[pl.ds(0, per_half * share), :], mine_out, out_own.at[0]).wait()
 
 
 def shards(n, groups, subs, q, k, v, weight, q_gain, k_gain, gate, count):
     tokens, features = q.shape
     width = weight.shape[1]
     share, per_half = width // MEMBERS, n // subs
-    vmem = pl.BlockSpec(memory_space=pltpu.VMEM)
     hbm = pl.BlockSpec(memory_space=pl.ANY)
     dma = pltpu.SemaphoreType.DMA
     rows = n * tokens
     return pl.pallas_call(
         functools.partial(kernel, n, math.isqrt(groups), subs),
         out_shape=jax.ShapeDtypeStruct((per_half * width, tokens), BF16),
-        in_specs=[hbm] * 4 + [vmem] * 3 + [pl.BlockSpec(memory_space=pltpu.SMEM)],
-        out_specs=vmem,
+        in_specs=[hbm] * 7 + [pl.BlockSpec(memory_space=pltpu.SMEM)],
+        out_specs=hbm,
         scratch_shapes=[
             pltpu.VMEM((tokens, features), BF16),
             pltpu.VMEM((tokens, features), BF16),
             pltpu.VMEM((tokens, features), BF16),
+            pltpu.VMEM((1, features), F32),
+            pltpu.VMEM((1, features), F32),
+            pltpu.VMEM((per_half * width,), F32),
             pltpu.VMEM((per_half * width, HD), F32),
             pltpu.VMEM((2, tokens, HD), F32),
             pltpu.VMEM((2, tokens, HD), F32),
@@ -380,15 +386,21 @@
             pltpu.VMEM((per_half * share, features), BF16),
             pltpu.VMEM((MEMBERS * per_half * share, HD), F32),
             pltpu.VMEM((MEMBERS * per_half * share, tokens), BF16),
-            dma((4,)),
-        ]
-        + [dma((n,))] * 8
-        + [dma((4, n // 2))] * 2
-        + [dma((per_half,))] * 2
-        + [dma((1,))] * 2
-        + [dma((per_half, MEMBERS))] * 2
-        + [dma((MEMBERS,))] * 4
-        + [dma((per_half, MEMBERS))] * 2,
+            dma((7,)),
+            dma((8,)),
+            dma((1,)),
+            dma((1,)),
+            dma((n,)),
+            dma((n,)),
+            dma((4, n // 2)),
+            dma((per_half,)),
+            dma((1,)),
+            dma((1,)),
+            dma((MEMBERS,)),
+            dma((MEMBERS,)),
+            dma((1,)),
+            dma((1,)),
+        ],
         compiler_params=pltpu.CompilerParams(
             collective_id=0, has_side_effects=True, vmem_limit_bytes=56 * 2**20
         ),

time: 187 us -> 176 us (0.941)
  Pallas kernels: 184 us -> 173 us
    pallas_call x1, Pallas kernels: 184 us -> 173 us  [shards(): pl.pallas_call(functools.partial(kernel, n, math.isqrt(groups), subs), ou...]
where the time goes in v3:
time: 176 us
  Pallas kernels  173 us (98%)
  local copies, waits for them, and re-layouts  2.16 us (1%)
    pallas_call x1, Pallas kernels, shards(): pl.pallas_call(functools.partial(kernel, n, math.isqrt(groups), subs), ou...  173 us

profile of v3, /device:TPU:69, one launch (start us, length us, event | category | flops | bytes accessed | tf_op | source)
XLA Modules:
  0.0 175.6 jit_solution(884985610677449803)
XLA Ops:
  0.7 172.8 %attention.1 = bf16[2560,128]{1,0:T(8,128)(2,1)} custom-call(bf16[128,2048]{1,0:T(8,128)(2,1)} %q_any.1, bf16[128,2048]{1,0:T(8,128)(2,1)} %k_any.1, bf16[128,2048]{1,0:T(8,128)(2,1)} %v_any.1, bf16[320,2048]{1,0:T(8,128)(2,1)} %bitcast.5, f32[1,2048]{1,0:T(1,128)} %bitcast.6, f32[1,2048]{1,0:T(1,128)} %bitcast.7, f32[2560]{0:T(1024)} %gate_any.1, ...), custom_call_target="tpu_custom_call" | custom-call | tf_op jit(solution)/shard_map/attention/pallas_call | solution.py:362
  173.4 2.2 %copy.9 = bf16[128,2560]{1,0:T(8,128)(2,1)} copy(bf16[128,2560]{0,1:T(8,128)(2,1)} %bitcast.4) | data formatting | bytes 1310720 | tf_op jit(solution)/shard_map/transpose | solution.py:408

commit v4 on v3

--- a/solution.py
+++ b/solution.py
@@ -13,8 +13,8 @@
 MEMBERS = 4
 CUTS = (48, 32)
 IN_ATTENTION = ((6, 0), (16, 1))
-IN_SQUARE = {0: 2}
-IN_PROJECTION = ((5, 3), (7, 4), (9, 5), (11, 6), (13, 7), (15, 8))
+IN_SQUARE = {1: 2}
+IN_PROJECTION = ((5, 3), (7, 4), (9, 5), (11, 6), (13, 7))
 F32, BF16 = jnp.float32, jnp.bfloat16
 
 
@@ -38,9 +38,9 @@
     q_any, k_any, v_any, w_any, q_gain_any, k_gain_any, gate_any, count,
     out,
     q_in, k_in, v_in, q_gain, k_gain, gate_in, gate_turned, squares, squares_in, kn, qn, k_all, v_all, q_all, bias, o_out,
-    att, w_ring, w_pair, gates, result,
+    att, w_ring, partial, other_partial, gates, result,
     load, sends, v_recv, k_recv, q_recv, o_recv,
-    ring_recv, w_recv, small_recv, gate_recv, att_recv, pair_recv, out_recv, out_own,
+    ring_recv, small_recv, gate_recv, att_recv, pair_recv, out_recv, out_own,
 ):
     tokens, features = q_in.shape
     share = w_any.shape[0] // MEMBERS
@@ -59,10 +59,13 @@
     def hop(i):
         return (i % 2) * ((i + 1) // 2) + (1 - i % 2) * ((n - i // 2) % n)
 
+    def far(i):
+        return hop((n - i) % n)
+
     barrier = pltpu.get_barrier_semaphore()
 
     def greet(i, carry):
-        pl.semaphore_signal(barrier, inc=1, device_id={"seq": (z + hop(n - i)) % n}, device_id_type=pl.DeviceIdType.MESH)
+        pl.semaphore_signal(barrier, inc=1, device_id={"seq": (z + far(i)) % n}, device_id_type=pl.DeviceIdType.MESH)
         return carry
 
     lax.fori_loop(1, n, greet, 0)
@@ -73,19 +76,11 @@
     loads = [
         pltpu.make_async_copy(source, target, load.at[index])
         for index, (source, target) in enumerate((
-            (k_any, k_in), (q_any, q_in), (v_any, v_in), (k_gain_any, k_gain), (q_gain_any, q_gain), (gate_any, gate_in),
+            (v_any, v_in), (k_any, k_in), (q_any, q_in), (k_gain_any, k_gain), (q_gain_any, q_gain), (gate_any, gate_in),
         ))
     ]
     for copy in loads:
         copy.start()
-
-    for index, array in enumerate((k_in, q_in)):
-        loads[index].wait()
-        total = jnp.zeros((tokens, HD), F32)
-        for head in range(features // HD):
-            wide = array[:, head * HD : (head + 1) * HD].astype(F32)
-            total = total + wide * wide
-        squares[index] = total
 
     weight_load = pltpu.make_async_copy(
         w_any.at[pl.ds(pl.multiple_of(me * share, 16), share), :],
@@ -94,12 +89,38 @@
     )
     weight_load.start()
 
-    loads[2].wait()
+    def ring(k, upwards, chunk):
+        plane = (z - k + n) % n if upwards else (z + k) % n
+        start = plane * share + sum(CUTS[:chunk])
+        rows = w_ring.at[pl.ds(pl.multiple_of(start, 16), CUTS[chunk]), :]
+        to = (z + 1) % n if upwards else (z + n - 1) % n
+        lane = 2 * chunk + upwards
+        return remote(rows, rows, sends.at[3], ring_recv.at[lane, k], {"seq": to})
+
+    ways = [(upwards, chunk, n // 2 - (upwards != (chunk == 0))) for chunk in (0, 1) for upwards in (True, False)]
+
+    def relay(k):
+        if k:
+            with jax.named_scope(f"relay{k}"):
+                for upwards, chunk, hops in ways:
+                    if k <= hops:
+                        ring_arrival(k, upwards, chunk).wait_recv()
+                    if k < hops:
+                        ring(k, upwards, chunk).start()
+        else:
+            for upwards, chunk, hops in ways:
+                ring(0, upwards, chunk).start()
+
+    def ring_arrival(k, upwards, chunk):
+        plane = (z - k + n) % n if upwards else (z + k) % n
+        start = plane * share + sum(CUTS[:chunk])
+        rows = w_ring.at[pl.ds(pl.multiple_of(start, 16), CUTS[chunk]), :]
+        lane = 2 * chunk + upwards
+        return remote(rows, rows, sends.at[3], ring_recv.at[lane, k - 1], {"seq": z})
+
+    loads[0].wait()
     with jax.named_scope("barrier"):
         pl.semaphore_wait(barrier, n - 1 + 1 + MEMBERS - 1)
-
-    pair = remote(squares, squares_in, sends.at[1], small_recv.at[0], {"sub": 1 - s})
-    pair.start()
 
     own = pl.ds(pl.multiple_of(z * tokens, tokens), tokens)
 
@@ -123,7 +144,19 @@
 
         lax.fori_loop(first, last, one, 0)
 
+    weight_load.wait()
     to_peers(0, 1, n)
+
+    for index, array in enumerate((k_in, q_in)):
+        loads[1 + index].wait()
+        total = jnp.zeros((tokens, HD), F32)
+        for head in range(features // HD):
+            wide = array[:, head * HD : (head + 1) * HD].astype(F32)
+            total = total + wide * wide
+        squares[index] = total
+
+    pair = remote(squares, squares_in, sends.at[1], small_recv.at[0], {"sub": 1 - s})
+    pair.start()
 
     loads[5].wait()
     gate = gate_in[...].reshape(1, gate_in.shape[0])
@@ -161,51 +194,6 @@
     positions = lax.broadcasted_iota(jnp.int32, bias.shape, 1)
     bias[...] = jnp.where(positions < count[0], 0.0, -1e30)
 
-    weight_load.wait()
-
-    def ring(k, upwards, chunk):
-        plane = (z - k + n) % n if upwards else (z + k) % n
-        start = plane * share + sum(CUTS[:chunk])
-        rows = w_ring.at[pl.ds(pl.multiple_of(start, 16), CUTS[chunk]), :]
-        to = (z + 1) % n if upwards else (z + n - 1) % n
-        lane = 2 * chunk + upwards
-        return remote(rows, rows, sends.at[3], ring_recv.at[lane, k], {"seq": to})
-
-    ways = [(upwards, chunk, n // 2 - (upwards != (chunk == 0))) for chunk in (0, 1) for upwards in (True, False)]
-
-    def pair_weights(plane):
-        row = pl.multiple_of((plane % per_half) * share, 16)
-        return remote(w_ring.at[pl.ds(pl.multiple_of(plane * share, 16), share), :], w_pair.at[pl.ds(row, share), :],
-                      sends.at[4], w_recv.at[plane % per_half], {"sub": 1 - s})
-
-    def have(plane):
-        @pl.when(plane // per_half != s)
-        def _():
-            pair_weights(plane).start()
-
-    def relay(k):
-        if k:
-            with jax.named_scope(f"relay{k}"):
-                for upwards, chunk, hops in ways:
-                    if k <= hops:
-                        ring_arrival(k, upwards, chunk).wait_recv()
-                    if k < hops:
-                        ring(k, upwards, chunk).start()
-            have((z + k) % n)
-            if 2 * k < n:
-                have((z - k + n) % n)
-        else:
-            for upwards, chunk, hops in ways:
-                ring(0, upwards, chunk).start()
-            have(z)
-
-    def ring_arrival(k, upwards, chunk):
-        plane = (z - k + n) % n if upwards else (z + k) % n
-        start = plane * share + sum(CUTS[:chunk])
-        rows = w_ring.at[pl.ds(pl.multiple_of(start, 16), CUTS[chunk]), :]
-        lane = 2 * chunk + upwards
-        return remote(rows, rows, sends.at[3], ring_recv.at[lane, k - 1], {"seq": z})
-
     def whole(array, arrive):
         there = array.at[pl.ds(0, (n - 1) * tokens), :]
         return remote(there, there, sends.at[0], arrive.at[0], {"seq": z})
@@ -214,7 +202,7 @@
         whole(v_all, v_recv).wait_recv()
         whole(k_all, k_recv).wait_recv()
     factor = math.log2(math.e) / math.sqrt(HD)
-    mine = pl.ds(pl.multiple_of((s * MEMBERS + me) * tokens, tokens), tokens)
+    mine = pl.ds(pl.multiple_of(me * tokens, tokens), tokens)
 
     def o_copy(d):
         lanes = pl.ds(pl.multiple_of(z * HD, HD), HD)
@@ -271,23 +259,12 @@
     with jax.named_scope("o"):
         lax.fori_loop(0, n, o_arrived, 0)
 
-    def block(half, number):
-        return att.at[pl.ds(pl.multiple_of((half * MEMBERS + number) * tokens, tokens), tokens), :]
-
-    pair_copies = {}
-    for e in range(MEMBERS):
-        number = square(e)[1]
-        pair_copies[e] = remote(block(s, number), block(s, number), sends.at[6], pair_recv.at[e], {"sub": 1 - s})
-        if e:
-            with jax.named_scope(f"square{e}"):
-                remote(block(s, number), block(s, number), sends.at[5], att_recv.at[e], {"sub": s}).wait_recv()
-        pair_copies[e].start()
+    for e in range(1, MEMBERS):
+        rows = att.at[pl.ds(pl.multiple_of(square(e)[1] * tokens, tokens), tokens), :]
+        with jax.named_scope(f"square{e}"):
+            remote(rows, rows, sends.at[5], att_recv.at[e], {"sub": s}).wait_recv()
         if e in IN_SQUARE:
             relay(IN_SQUARE[e])
-    for e in range(MEMBERS):
-        with jax.named_scope(f"pair{e}"):
-            pair_copies[e].wait_recv()
-
     others = (MEMBERS - 1) * per_half * share
 
     def all_gates():
@@ -296,15 +273,17 @@
 
     all_gates().wait_recv()
 
-    every = MEMBERS * tokens
-
-    def half_att(half):
-        return att[pl.ds(pl.multiple_of(half * every, HD), every), :]
+    def place(i):
+        return pl.ds(pl.multiple_of(i * share, 16), share)
+
+    def give(i):
+        return remote(partial.at[1, place(i), :], other_partial.at[place(i), :],
+                      sends.at[4], pair_recv.at[i], {"sub": 1 - s})
 
     def out_copy(i, e):
         there, number = square(e)
         return remote(result.at[pl.ds(pl.multiple_of((number * per_half + i) * share, 16), share), :],
-                      out.at[gate_rows(i, me), :], sends.at[7], out_recv.at[0], {"groups": there})
+                      out.at[gate_rows(i, me), :], sends.at[6], out_recv.at[0], {"groups": there})
 
     def own_out(i):
         rows = pl.ds(pl.multiple_of((me * per_half + i) * share, 16), share)
@@ -313,41 +292,60 @@
     def project(j, carry):
         plane = (z + hop(j)) % n
         i = plane % per_half
+        mine = plane // per_half == s
+        with jax.named_scope("project"):
+            total = nt(w_ring[pl.ds(pl.multiple_of(plane * share, 16), share), :], att[...])
+            partial[jnp.where(mine, 0, 1), place(i), :] = total
+
+        @pl.when(jnp.logical_not(mine))
+        def _():
+            give(i).start()
+
+        @pl.when((j >= 2) & (j < n - 1))
+        def _():
+            finish(j - 2)
+
+        return carry
+
+    def finish(j):
+        plane = (z + hop(j)) % n
+        i = plane % per_half
 
         @pl.when(plane // per_half == s)
         def _():
-            with jax.named_scope("pairw"):
-                pair_weights(plane).wait_recv()
-            with jax.named_scope("project"):
-                total = nt(w_ring[pl.ds(pl.multiple_of(plane * share, 16), share), :], half_att(s))
-                total = total + nt(w_pair[pl.ds(pl.multiple_of(i * share, 16), share), :], half_att(1 - s))
-                for number in range(MEMBERS):
-                    rows = pl.ds(pl.multiple_of((number * per_half + i) * share, 16), share)
-                    result[rows, :] = (total[:, number * tokens : (number + 1) * tokens] * gates[rows, :]).astype(BF16)
+            with jax.named_scope("pair"):
+                give(i).wait_recv()
+            for number in range(MEMBERS):
+                rows = pl.ds(pl.multiple_of((number * per_half + i) * share, 16), share)
+                lanes = slice(number * tokens, (number + 1) * tokens)
+                total = partial[0, place(i), lanes] + other_partial[place(i), lanes]
+                result[rows, :] = (total * gates[rows, :]).astype(BF16)
             for e in range(1, MEMBERS):
                 out_copy(i, e).start()
             own_out(i).start()
 
-        return carry
-
-    spread(project, 0, n, IN_PROJECTION)
+    spread(project, 0, n - 1, IN_PROJECTION)
+    finish(n - 3)
+    finish(n - 2)
+    relay(n // 2)
+    project(n - 1, 0)
+    finish(n - 1)
 
     def all_sent(array, rows, index):
         there = array.at[pl.ds(0, rows), :]
         remote(there, there, sends.at[index], small_recv.at[0], {"seq": z}).wait_send()
 
     peers = (n - 1) * tokens * HD // features
-    all_sent(att, 4 * peers, 0)
+    all_sent(w_ring, 4 * peers, 0)
     pair.wait_send()
     all_gates().wait_send()
     all_sent(w_ring, (n - 1) * share, 3)
-    all_sent(w_pair, per_half * share, 4)
+    all_sent(other_partial, per_half * share, 4)
     all_sent(att, (MEMBERS - 1) * tokens, 5)
-    all_sent(att, MEMBERS * tokens, 6)
-    all_sent(result, others, 7)
+    all_sent(result, others, 6)
     with jax.named_scope("out"):
         there = out.at[pl.ds(0, others), :]
-        remote(there, there, sends.at[7], out_recv.at[0], {"seq": z}).wait_recv()
+        remote(there, there, sends.at[6], out_recv.at[0], {"seq": z}).wait_recv()
         mine_out = out.at[pl.ds(0, per_half * share), :]
         pltpu.make_async_copy(result.at[pl.ds(0, per_half * share), :], mine_out, out_own.at[0]).wait()
 
@@ -381,23 +379,23 @@
             pltpu.VMEM((rows, HD), BF16),
             pltpu.VMEM((8, rows), F32),
             pltpu.VMEM((n, tokens, HD), BF16),
-            pltpu.VMEM((subs * MEMBERS * tokens, features), BF16),
+            pltpu.VMEM((MEMBERS * tokens, features), BF16),
             pltpu.VMEM((n * share, features), BF16),
-            pltpu.VMEM((per_half * share, features), BF16),
+            pltpu.VMEM((2, per_half * share, MEMBERS * tokens), F32),
+            pltpu.VMEM((per_half * share, MEMBERS * tokens), F32),
             pltpu.VMEM((MEMBERS * per_half * share, HD), F32),
             pltpu.VMEM((MEMBERS * per_half * share, tokens), BF16),
             dma((7,)),
-            dma((8,)),
+            dma((7,)),
             dma((1,)),
             dma((1,)),
             dma((n,)),
             dma((n,)),
             dma((4, n // 2)),
+            dma((1,)),
+            dma((1,)),
+            dma((MEMBERS,)),
             dma((per_half,)),
-            dma((1,)),
-            dma((1,)),
-            dma((MEMBERS,)),
-            dma((MEMBERS,)),
             dma((1,)),
             dma((1,)),
         ],

time: 176 us -> 172 us (0.977)
  Pallas kernels: 173 us -> 169 us
    pallas_call x1, Pallas kernels: 173 us -> 169 us  [shards(): pl.pallas_call(functools.partial(kernel, n, math.isqrt(groups), subs), ou...]
where the time goes in v4:
time: 172 us
  Pallas kernels  169 us (98%)
  local copies, waits for them, and re-layouts  2.16 us (1%)
    pallas_call x1, Pallas kernels, shards(): pl.pallas_call(functools.partial(kernel, n, math.isqrt(groups), subs), ou...  169 us

profile of v4, /device:TPU:69, one launch (start us, length us, event | category | flops | bytes accessed | tf_op | source)
XLA Modules:
  0.0 172.3 jit_solution(7016495331355993942)
XLA Ops:
  0.7 169.4 %attention.1 = bf16[2560,128]{1,0:T(8,128)(2,1)} custom-call(bf16[128,2048]{1,0:T(8,128)(2,1)} %q_any.1, bf16[128,2048]{1,0:T(8,128)(2,1)} %k_any.1, bf16[128,2048]{1,0:T(8,128)(2,1)} %v_any.1, bf16[320,2048]{1,0:T(8,128)(2,1)} %bitcast.5, f32[1,2048]{1,0:T(1,128)} %bitcast.6, f32[1,2048]{1,0:T(1,128)} %bitcast.7, f32[2560]{0:T(1024)} %gate_any.1, ...), custom_call_target="tpu_custom_call" | custom-call | tf_op jit(solution)/shard_map/attention/pallas_call | solution.py:360
  170.1 2.2 %copy.9 = bf16[128,2560]{1,0:T(8,128)(2,1)} copy(bf16[128,2560]{0,1:T(8,128)(2,1)} %bitcast.4) | data formatting | bytes 1310720 | tf_op jit(solution)/shard_map/transpose | solution.py:406

commit v5 on v4

--- a/solution.py
+++ b/solution.py
@@ -39,7 +39,7 @@
     out,
     q_in, k_in, v_in, q_gain, k_gain, gate_in, gate_turned, squares, squares_in, kn, qn, k_all, v_all, q_all, bias, o_out,
     att, w_ring, partial, other_partial, gates, result,
-    load, sends, v_recv, k_recv, q_recv, o_recv,
+    from_up, from_down, load, sends, v_recv, k_recv, q_recv, o_recv,
     ring_recv, small_recv, gate_recv, att_recv, pair_recv, out_recv, out_own,
 ):
     tokens, features = q_in.shape
@@ -64,11 +64,13 @@
 
     barrier = pltpu.get_barrier_semaphore()
 
+    near = n // 4
+
     def greet(i, carry):
         pl.semaphore_signal(barrier, inc=1, device_id={"seq": (z + far(i)) % n}, device_id_type=pl.DeviceIdType.MESH)
         return carry
 
-    lax.fori_loop(1, n, greet, 0)
+    lax.fori_loop(n - 2 * near, n, greet, 0)
     pl.semaphore_signal(barrier, inc=1, device_id={"sub": 1 - s}, device_id_type=pl.DeviceIdType.MESH)
     for e in range(1, MEMBERS):
         pl.semaphore_signal(barrier, inc=1, device_id={"groups": square(e)[0]}, device_id_type=pl.DeviceIdType.MESH)
@@ -120,7 +122,7 @@
 
     loads[0].wait()
     with jax.named_scope("barrier"):
-        pl.semaphore_wait(barrier, n - 1 + 1 + MEMBERS - 1)
+        pl.semaphore_wait(barrier, 2 * near + 1 + MEMBERS - 1)
 
     own = pl.ds(pl.multiple_of(z * tokens, tokens), tokens)
 
@@ -145,7 +147,13 @@
         lax.fori_loop(first, last, one, 0)
 
     weight_load.wait()
-    to_peers(0, 1, n)
+    pl.semaphore_signal(from_down.at[0], inc=1, device_id={"seq": (z + near) % n}, device_id_type=pl.DeviceIdType.MESH)
+    pl.semaphore_signal(from_up.at[0], inc=1, device_id={"seq": (z + n - near) % n}, device_id_type=pl.DeviceIdType.MESH)
+    to_peers(0, 1, 1 + 2 * near)
+    with jax.named_scope("beyond"):
+        pl.semaphore_wait(from_down.at[0], 1)
+        pl.semaphore_wait(from_up.at[0], 1)
+    to_peers(0, 1 + 2 * near, n)
 
     for index, array in enumerate((k_in, q_in)):
         loads[1 + index].wait()
@@ -325,11 +333,10 @@
             own_out(i).start()
 
     spread(project, 0, n - 1, IN_PROJECTION)
-    finish(n - 3)
-    finish(n - 2)
     relay(n // 2)
     project(n - 1, 0)
-    finish(n - 1)
+    for j in (3, 2, 1):
+        finish(n - j)
 
     def all_sent(array, rows, index):
         there = array.at[pl.ds(0, rows), :]
@@ -385,6 +392,8 @@
             pltpu.VMEM((per_half * share, MEMBERS * tokens), F32),
             pltpu.VMEM((MEMBERS * per_half * share, HD), F32),
             pltpu.VMEM((MEMBERS * per_half * share, tokens), BF16),
+            pltpu.SemaphoreType.REGULAR((1,)),
+            pltpu.SemaphoreType.REGULAR((1,)),
             dma((7,)),
             dma((7,)),
             dma((1,)),

time: 172 us -> 171 us (level)
    pallas_call x1, Pallas kernels: 169 us -> 168 us  [shards(): pl.pallas_call(functools.partial(kernel, n, math.isqrt(groups), subs), ou...]
where the time goes in v5:
time: 171 us; the launch traced here: 170 us
  Pallas kernels  168 us (98%)
  local copies, waits for them, and re-layouts  2.16 us (1%)
    pallas_call x1, Pallas kernels, shards(): pl.pallas_call(functools.partial(kernel, n, math.isqrt(groups), subs), ou...  168 us

profile of v5, /device:TPU:69, one launch (start us, length us, event | category | flops | bytes accessed | tf_op | source)
XLA Modules:
  0.0 170.4 jit_solution(13609669008694348531)
XLA Ops:
  0.7 167.5 %attention.1 = bf16[2560,128]{1,0:T(8,128)(2,1)} custom-call(bf16[128,2048]{1,0:T(8,128)(2,1)} %q_any.1, bf16[128,2048]{1,0:T(8,128)(2,1)} %k_any.1, bf16[128,2048]{1,0:T(8,128)(2,1)} %v_any.1, bf16[320,2048]{1,0:T(8,128)(2,1)} %bitcast.5, f32[1,2048]{1,0:T(1,128)} %bitcast.6, f32[1,2048]{1,0:T(1,128)} %bitcast.7, f32[2560]{0:T(1024)} %gate_any.1, ...), custom_call_target="tpu_custom_call" | custom-call | tf_op jit(solution)/shard_map/attention/pallas_call | solution.py:367
  168.2 2.2 %copy.9 = bf16[128,2560]{1,0:T(8,128)(2,1)} copy(bf16[128,2560]{0,1:T(8,128)(2,1)} %bitcast.4) | data formatting | bytes 1310720 | tf_op jit(solution)/shard_map/transpose | solution.py:415

commit v6 on v5

--- a/solution.py
+++ b/solution.py
@@ -40,7 +40,7 @@
     q_in, k_in, v_in, q_gain, k_gain, gate_in, gate_turned, squares, squares_in, kn, qn, k_all, v_all, q_all, bias, o_out,
     att, w_ring, partial, other_partial, gates, result,
     from_up, from_down, load, sends, v_recv, k_recv, q_recv, o_recv,
-    ring_recv, small_recv, gate_recv, att_recv, pair_recv, out_recv, out_own,
+    ring_recv, small_recv, gate_recv, att_recv, pair_recv, out_recv,
 ):
     tokens, features = q_in.shape
     share = w_any.shape[0] // MEMBERS
@@ -293,10 +293,6 @@
         return remote(result.at[pl.ds(pl.multiple_of((number * per_half + i) * share, 16), share), :],
                       out.at[gate_rows(i, me), :], sends.at[6], out_recv.at[0], {"groups": there})
 
-    def own_out(i):
-        rows = pl.ds(pl.multiple_of((me * per_half + i) * share, 16), share)
-        return pltpu.make_async_copy(result.at[rows, :], out.at[gate_rows(i, me), :], out_own.at[0])
-
     def project(j, carry):
         plane = (z + hop(j)) % n
         i = plane % per_half
@@ -330,7 +326,7 @@
                 result[rows, :] = (total * gates[rows, :]).astype(BF16)
             for e in range(1, MEMBERS):
                 out_copy(i, e).start()
-            own_out(i).start()
+            out[gate_rows(i, me), :] = result[pl.ds(pl.multiple_of((me * per_half + i) * share, 16), share), :]
 
     spread(project, 0, n - 1, IN_PROJECTION)
     relay(n // 2)
@@ -353,8 +349,6 @@
     with jax.named_scope("out"):
         there = out.at[pl.ds(0, others), :]
         remote(there, there, sends.at[6], out_recv.at[0], {"seq": z}).wait_recv()
-        mine_out = out.at[pl.ds(0, per_half * share), :]
-        pltpu.make_async_copy(result.at[pl.ds(0, per_half * share), :], mine_out, out_own.at[0]).wait()
 
 
 def shards(n, groups, subs, q, k, v, weight, q_gain, k_gain, gate, count):
@@ -368,7 +362,7 @@
         functools.partial(kernel, n, math.isqrt(groups), subs),
         out_shape=jax.ShapeDtypeStruct((per_half * width, tokens), BF16),
         in_specs=[hbm] * 7 + [pl.BlockSpec(memory_space=pltpu.SMEM)],
-        out_specs=hbm,
+        out_specs=pl.BlockSpec(memory_space=pltpu.VMEM),
         scratch_shapes=[
             pltpu.VMEM((tokens, features), BF16),
             pltpu.VMEM((tokens, features), BF16),
@@ -406,13 +400,12 @@
             dma((MEMBERS,)),
             dma((per_half,)),
             dma((1,)),
-            dma((1,)),
         ],
         compiler_params=pltpu.CompilerParams(
-            collective_id=0, has_side_effects=True, vmem_limit_bytes=56 * 2**20
+            collective_id=0, has_side_effects=True, vmem_limit_bytes=40 * 2**20
         ),
         name="attention",
-    )(q, k, v, weight.T, q_gain.reshape(1, -1), k_gain.reshape(1, -1), gate, count).T
+    )(*(pltpu.with_memory_space_constraint(x, pltpu.HBM) for x in (q, k, v, weight.T, q_gain.reshape(1, -1), k_gain.reshape(1, -1), gate)), count).T
 
 
 def solution(mesh):

time: 171 us -> 169 us (0.988)
  no operation moved by 1% of the time
where the time goes in v6:
time: 169 us
  Pallas kernels  167 us (99%)
    pallas_call x1, Pallas kernels, shards(): pl.pallas_call(functools.partial(kernel, n, math.isqrt(groups), subs), ou...  167 us

profile of v6, /device:TPU:69, one launch (start us, length us, event | category | flops | bytes accessed | tf_op | source)
XLA Modules:
  0.0 169.2 jit_solution(7453867985573820299)
XLA Ops:
  0.7 167.4 %attention.1 = bf16[2560,128]{1,0:T(8,128)(2,1)S(1)} custom-call(bf16[128,2048]{1,0:T(8,128)(2,1)} %q_any.1, bf16[128,2048]{1,0:T(8,128)(2,1)} %k_any.1, bf16[128,2048]{1,0:T(8,128)(2,1)} %v_any.1, bf16[320,2048]{1,0:T(8,128)(2,1)} %bitcast.5, f32[1,2048]{1,0:T(1,128)} %bitcast.6, f32[1,2048]{1,0:T(1,128)} %bitcast.7, f32[2560]{0:T(1024)} %gate_any.1, ...), custom_call_target="tpu_custom_call" | custom-call | tf_op jit(solution)/shard_map/attention/pallas_call | solution.py:361
  168.1 1.1 copy.9

commit v7 on v6

--- a/solution.py
+++ b/solution.py
@@ -12,7 +12,7 @@
 EPSILON = 1e-06
 MEMBERS = 4
 CUTS = (48, 32)
-IN_ATTENTION = ((6, 0), (16, 1))
+IN_ATTENTION = ((1, 0), (16, 1))
 IN_SQUARE = {1: 2}
 IN_PROJECTION = ((5, 3), (7, 4), (9, 5), (11, 6), (13, 7))
 F32, BF16 = jnp.float32, jnp.bfloat16
@@ -64,7 +64,7 @@
 
     barrier = pltpu.get_barrier_semaphore()
 
-    near = n // 4
+    near = n // 8
 
     def greet(i, carry):
         pl.semaphore_signal(barrier, inc=1, device_id={"seq": (z + far(i)) % n}, device_id_type=pl.DeviceIdType.MESH)
@@ -147,13 +147,14 @@
         lax.fori_loop(first, last, one, 0)
 
     weight_load.wait()
-    pl.semaphore_signal(from_down.at[0], inc=1, device_id={"seq": (z + near) % n}, device_id_type=pl.DeviceIdType.MESH)
-    pl.semaphore_signal(from_up.at[0], inc=1, device_id={"seq": (z + n - near) % n}, device_id_type=pl.DeviceIdType.MESH)
-    to_peers(0, 1, 1 + 2 * near)
-    with jax.named_scope("beyond"):
-        pl.semaphore_wait(from_down.at[0], 1)
-        pl.semaphore_wait(from_up.at[0], 1)
-    to_peers(0, 1 + 2 * near, n)
+    for known in range(near, n // 2, near):
+        pl.semaphore_signal(from_down.at[0], inc=1, device_id={"seq": (z + near) % n}, device_id_type=pl.DeviceIdType.MESH)
+        pl.semaphore_signal(from_up.at[0], inc=1, device_id={"seq": (z + n - near) % n}, device_id_type=pl.DeviceIdType.MESH)
+        to_peers(0, 1 + 2 * (known - near), 1 + 2 * known)
+        with jax.named_scope("beyond"):
+            pl.semaphore_wait(from_down.at[0], 1)
+            pl.semaphore_wait(from_up.at[0], 1)
+    to_peers(0, 1 + 2 * (n // 2 - near), n)
 
     for index, array in enumerate((k_in, q_in)):
         loads[1 + index].wait()

time: 169 us -> 169 us (level)
  no operation moved by 1% of the time
where the time goes in v7:
time: 169 us
  Pallas kernels  167 us (99%)
    pallas_call x1, Pallas kernels, shards(): pl.pallas_call(functools.partial(kernel, n, math.isqrt(groups), subs), ou...  167 us

profile of v7, /device:TPU:69, one launch (start us, length us, event | category | flops | bytes accessed | tf_op | source)
XLA Modules:
  0.0 168.6 jit_solution(16752548340987019960)
XLA Ops:
  0.7 166.9 %attention.1 = bf16[2560,128]{1,0:T(8,128)(2,1)S(1)} custom-call(bf16[128,2048]{1,0:T(8,128)(2,1)} %q_any.1, bf16[128,2048]{1,0:T(8,128)(2,1)} %k_any.1, bf16[128,2048]{1,0:T(8,128)(2,1)} %v_any.1, bf16[320,2048]{1,0:T(8,128)(2,1)} %bitcast.5, f32[1,2048]{1,0:T(1,128)} %bitcast.6, f32[1,2048]{1,0:T(1,128)} %bitcast.7, f32[2560]{0:T(1024)} %gate_any.1, ...), custom_call_target="tpu_custom_call" | custom-call | tf_op jit(solution)/shard_map/attention/pallas_call | solution.py:362
  167.6 1.1 copy.9

commit v8 on v7

--- a/solution.py
+++ b/solution.py
@@ -12,7 +12,8 @@
 EPSILON = 1e-06
 MEMBERS = 4
 CUTS = (48, 32)
-IN_ATTENTION = ((1, 0), (16, 1))
+IN_ATTENTION = ((1, 0),)
+IN_RETURN = ((6, 1),)
 IN_SQUARE = {1: 2}
 IN_PROJECTION = ((5, 3), (7, 4), (9, 5), (11, 6), (13, 7))
 F32, BF16 = jnp.float32, jnp.bfloat16
@@ -266,7 +267,7 @@
         return carry
 
     with jax.named_scope("o"):
-        lax.fori_loop(0, n, o_arrived, 0)
+        spread(o_arrived, 0, n, IN_RETURN)
 
     for e in range(1, MEMBERS):
         rows = att.at[pl.ds(pl.multiple_of(square(e)[1] * tokens, tokens), tokens), :]

time: 169 us -> 169 us (level)
  no operation moved by 1% of the time
where the time goes in v8:
time: 169 us
  Pallas kernels  167 us (99%)
    pallas_call x1, Pallas kernels, shards(): pl.pallas_call(functools.partial(kernel, n, math.isqrt(groups), subs), ou...  167 us

profile of v8, /device:TPU:69, one launch (start us, length us, event | category | flops | bytes accessed | tf_op | source)
XLA Modules:
  0.0 168.6 jit_solution(16494228952828863630)
XLA Ops:
  0.7 166.9 %attention.1 = bf16[2560,128]{1,0:T(8,128)(2,1)S(1)} custom-call(bf16[128,2048]{1,0:T(8,128)(2,1)} %q_any.1, bf16[128,2048]{1,0:T(8,128)(2,1)} %k_any.1, bf16[128,2048]{1,0:T(8,128)(2,1)} %v_any.1, bf16[320,2048]{1,0:T(8,128)(2,1)} %bitcast.5, f32[1,2048]{1,0:T(1,128)} %bitcast.6, f32[1,2048]{1,0:T(1,128)} %bitcast.7, f32[2560]{0:T(1024)} %gate_any.1, ...), custom_call_target="tpu_custom_call" | custom-call | tf_op jit(solution)/shard_map/attention/pallas_call | solution.py:363
  167.6 1.1 copy.9
